TPU v7x, 128 devices: a whole 4x4x4 slice. The times are simulated.
128 devices in a mesh: row: 8 (over z, core), col: 16 (over y, x).
Axes of the slice: x: 4, y: 4, z: 4, core: 2. Of those that a mesh axis runs over, the one named last changes fastest.
Arguments:
- clean: float32 [1344, 16384], P('row', 'col'), may hold values from -6 to 6
- noise: float32 [1344, 16384], P('row', 'col'), may hold values from -6 to 6
- bucket: int32 [64], replicated, may hold values from 0 to 31
- mod_table: float32 [1, 32, 1344], replicated, may hold values from -3 to 3
- w_first: float32 [1, 1344, 1344], P(None, 'row', 'col'), may hold values from -0.15625 to 0.15625
- w_second: float32 [1, 1344, 1344], P(None, 'col', 'row'), may hold values from -0.15625 to 0.15625
Outputs:
- grad_first: float32 [1, 1344, 1344], P(None, 'row', 'col')
- grad_second: float32 [1, 1344, 1344], P(None, 'col', 'row')
All inputs are finite; a program needn't handle non-finite values.
Results may differ from a plain program's by a relative error of at most 0.018.
Values may be sent and summed in bfloat16 or wider, within the bound.
A program may use at most 64 MiB of HBM per device.

v0:
```python
import math

import jax
import jax.numpy as jnp
from jax import lax
from jax.sharding import Mesh
from jax.sharding import PartitionSpec as P

PIX = 256
BUCKETS = 32
COL = ("col_0", "col_1")


MIX_WEIGHT = 0.3
KEEP_COEF = (1.0 - MIX_WEIGHT) / math.sqrt((1.0 - MIX_WEIGHT) ** 2 + MIX_WEIGHT**2)
ADD_COEF = MIX_WEIGHT / math.sqrt((1.0 - MIX_WEIGHT) ** 2 + MIX_WEIGHT**2)
SILU_GAIN = 1.0 / 0.596
CONTRACT_LEAD = (((0,), (0,)), ((), ()))
CONTRACT_TAIL = (((1,), (1,)), ((), ()))


def sent_to_all(value, axis):
    copies = jnp.broadcast_to(value, (lax.axis_size(axis), *value.shape))
    return lax.all_to_all(copies, axis, split_axis=0, concat_axis=0, tiled=True)


def over_copies(value, axis):
    everything = sent_to_all(value, axis)
    return jnp.sum(everything, axis=0)


def one_axis_at_a_time(value, axes):
    for axis in axes:
        value = lax.psum(value, axis)
    return value


def rows_first(arrays, axis, dims):
    turned = [jnp.moveaxis(a, dim, 0) for a, dim in zip(arrays, dims)]
    widths = [t[0].size for t in turned]
    both = jnp.concatenate([t.reshape(-1, w) for t, w in zip(turned, widths)], axis=1)
    result = lax.all_gather(both, axis, axis=0, tiled=True)
    blocks = jnp.split(result, [sum(widths[:k]) for k in range(1, len(widths))], axis=1)
    return tuple(
        (
            jnp.moveaxis(b.reshape(-1, *t.shape[1:]), 0, dim)
            for b, t, dim in zip(blocks, turned, dims)
        )
    )


def split_up(value, dim, count):
    before, after = (value.shape[:dim], value.shape[dim + 1 :])
    return jnp.moveaxis(value.reshape(*before, count, -1, *after), dim, 0)


def sum_together(arrays, axis, dims):
    count = lax.axis_size(axis)
    blocks = [split_up(a, dim, count) for a, dim in zip(arrays, dims)]
    lines = jnp.concatenate([b.reshape(count, -1) for b in blocks], axis=1)
    extent = max(16, -(-lines.shape[1] // 1024) * 8)
    lines = jnp.pad(lines, ((0, 0), (0, extent * 128 - lines.shape[1]))).reshape(-1, 128)
    ravelled, at, gathered = (lax.psum_scatter(lines, axis, tiled=True).reshape(-1), 0, [])
    for b in blocks:
        part = b[0]
        gathered.append(ravelled[at : at + part.size].reshape(part.shape))
        at += part.size
    return tuple(gathered)


def noise_levels(bucket):
    return jnp.exp(-3.0 + 5.0 * (bucket.astype(jnp.float32) + 0.5) / BUCKETS)


def silu_slope(values):
    sig = jax.nn.sigmoid(values)
    return sig * (1.0 + values * (1.0 - sig))


def bucket_gains(table, picked):
    onehot = (picked[:, None] == jnp.arange(table.shape[0], dtype=jnp.int32)[None, :]).astype(
        jnp.float32
    )
    return jnp.dot(onehot, table, preferred_element_type=jnp.float32)


def local(clean, noise, bucket, mod_table, w_first, w_second):
    rows_size = lax.axis_size("row")
    row_at = lax.axis_index("row")
    col_at = lax.axis_index(COL)
    samples = bucket.shape[0]
    own_rows = clean.shape[1]
    weight_first = w_first[0]
    weight_second = w_second[0]
    table = 1.0 + mod_table[0]
    col_first = jnp.sqrt(over_copies(jnp.sum(weight_first * weight_first, axis=0), "row") + 1.0)
    col_second = jnp.sqrt(
        one_axis_at_a_time(jnp.sum(weight_second * weight_second, axis=0), COL) + 1.0
    )
    normed_first = (weight_first / col_first[None, :]).astype(jnp.bfloat16)
    normed_second = (weight_second / col_second[None, :]).astype(jnp.bfloat16)
    chan_clean, chan_noise = (
        lax.all_to_all(
            clean.astype(jnp.bfloat16), "row", split_axis=1, concat_axis=0, tiled=True
        ).astype(clean.dtype),
        lax.all_to_all(
            noise.astype(jnp.bfloat16), "row", split_axis=1, concat_axis=0, tiled=True
        ).astype(noise.dtype),
    )
    local_clean = chan_clean.T
    local_noise = chan_noise.T
    sub_rows = own_rows // rows_size
    first_row = col_at * own_rows + row_at * sub_rows
    row_sample = (first_row + jnp.arange(sub_rows, dtype=jnp.int32)) // PIX
    row_bucket = jnp.take(bucket, row_sample)
    levels = noise_levels(row_bucket)[:, None]
    spread_root = jnp.sqrt(levels * levels + 0.25)
    state_own = ((local_clean + levels * local_noise) / spread_root).astype(jnp.bfloat16)
    target = local_clean * (2.0 * levels / spread_root) - local_noise * (0.5 / spread_root)
    gains = bucket_gains(table, row_bucket)
    part_first, part_second = rows_first((normed_first, normed_second), COL, (1, 0))
    full_first, full_second = rows_first((part_first, part_second), "row", (0, 1))
    pre_act = jnp.dot(state_own, full_first, preferred_element_type=jnp.float32)
    hidden = (jax.nn.silu(pre_act) * SILU_GAIN * gains).astype(jnp.bfloat16)
    branch = jnp.dot(hidden, full_second, preferred_element_type=jnp.float32)
    state_new = (KEEP_COEF * state_own.astype(jnp.float32) + ADD_COEF * branch).astype(jnp.bfloat16)
    grad_own = (state_new.astype(jnp.float32) - target) / samples
    dbranch = (ADD_COEF * grad_own).astype(jnp.bfloat16)
    gsecond_full = lax.dot_general(
        hidden, dbranch, CONTRACT_LEAD, preferred_element_type=jnp.float32
    )
    dhidden = lax.dot_general(
        dbranch, full_second, CONTRACT_TAIL, preferred_element_type=jnp.float32
    )
    dpre = (dhidden * gains * silu_slope(pre_act) * SILU_GAIN).astype(jnp.bfloat16)
    gfirst_full = lax.dot_general(
        state_own, dpre, CONTRACT_LEAD, preferred_element_type=jnp.float32
    )
    part_gfirst, part_gsecond = (
        lax.psum_scatter(
            gfirst_full.astype(jnp.bfloat16), COL, scatter_dimension=1, tiled=True
        ).astype(jnp.float32),
        lax.psum_scatter(
            gsecond_full.astype(jnp.bfloat16), COL, scatter_dimension=0, tiled=True
        ).astype(jnp.float32),
    )
    gfirst, gsecond = tuple(
        (
            part.astype(jnp.float32)
            for part in sum_together(
                (part_gfirst.astype(jnp.bfloat16), part_gsecond.astype(jnp.bfloat16)), "row", (0, 1)
            )
        )
    )
    dot_first = over_copies(jnp.sum(weight_first * gfirst, axis=0), "row")
    dot_second = one_axis_at_a_time(jnp.sum(weight_second * gsecond, axis=0), COL)
    grad_first = gfirst / col_first[None, :] - weight_first * (dot_first / col_first**3)[None, :]
    grad_second = (
        gsecond / col_second[None, :] - weight_second * (dot_second / col_second**3)[None, :]
    )
    return (grad_first[None], grad_second[None])


def solution(mesh):
    torus = Mesh(mesh.devices.reshape(mesh.shape["row"], 4, 4), ("row", "col_0", "col_1"))
    in_specs = (P("row", COL), P("row", COL), P(), P(), P(None, "row", COL), P(None, COL, "row"))
    out_specs = (P(None, "row", COL), P(None, COL, "row"))
    return jax.shard_map(local, mesh=torus, in_specs=in_specs, out_specs=out_specs, check_vma=False)
```

profile of v0, /device:TPU:1, one launch (start us, length us, event | category | flops | bytes accessed | tf_op | source)
XLA Modules:
  0.0 332.8 jit_solution(9308178163140917538)
XLA Ops:
  8.7 6.8 %all-to-all-start.2 = ((f32[8,1,84]{2,1,0:T(1,128)}), f32[8,1,84]{2,1,0:T(1,128)S(1)}, u32[]{:S(2)}, u32[]{:S(2)}) async-start(f32[8,1,84]{2,1,0:T(1,128)} %broadcast_in_dim.11), calls=%async_computation.2 | async-start | bytes 8192 | tf_op jit(solution)/shard_map/all_to_all | solution.py:24
  16.6 8.7 %psum.28 = f32[168]{0:T(256)S(1)} all-reduce(f32[168]{0:T(256)S(1)} %fusion.60), channel_id=1, replica_groups=mesh['row'=8,'col_0'=4,'col_1'=4] {'col_0'}, use_global_device_ids=true, to_apply=%region_3.0 | all-reduce | flops 168 | bytes 1344 | tf_op jit(solution)/shard_map/psum | solution.py:34
  25.3 8.5 %psum.29 = f32[168]{0:T(256)S(1)} all-reduce(f32[168]{0:T(256)S(1)} %psum.28), channel_id=1, replica_groups=mesh['row'=8,'col_0'=4,'col_1'=4] {'col_1'}, use_global_device_ids=true, to_apply=%region_4.0 | all-reduce | flops 168 | bytes 1344 | tf_op jit(solution)/shard_map/psum | solution.py:34
  35.0 17.3 %all-gather = bf16[16,84,336]{2,1,0:T(8,128)(2,1)S(1)} all-gather(bf16[1,84,336]{2,1,0:T(8,128)(2,1)S(1)} %copy.38), channel_id=1, replica_groups=mesh['row'=8,'col_0'=4,'col_1'=4] {'col_0','col_1'}, dimensions={0}, use_global_device_ids=true | all-gather | bytes 959616 | tf_op jit(solution)/shard_map/all_gather | solution.py:42
  55.9 13.5 %all-to-all-start = ((bf16[168,8,128]{2,0,1:T(8,128)(2,1)}), bf16[168,8,128]{2,0,1:T(8,128)(2,1)S(1)}, u32[]{:S(2)}, u32[]{:S(2)}) async-start(bf16[168,8,128]{2,0,1:T(8,128)(2,1)} %copy_bitcast_fusion.2), calls=%async_computation | async-start | bytes 688128 | tf_op jit(solution)/shard_map/all_to_all | solution.py:103
  71.5 5.1 %all-to-all-done = bf16[168,8,128]{2,0,1:T(8,128)(2,1)S(1)} async-done(((bf16[168,8,128]{2,0,1:T(8,128)(2,1)}), bf16[168,8,128]{2,0,1:T(8,128)(2,1)S(1)}, u32[]{:S(2)}, u32[]{:S(2)}) %all-to-all-start) | async-done | bytes 344096 | tf_op jit(solution)/shard_map/all_to_all | solution.py:103
  76.6 4.5 %all-to-all-start.1 = ((bf16[168,8,128]{2,0,1:T(8,128)(2,1)}), bf16[168,8,128]{2,0,1:T(8,128)(2,1)S(1)}, u32[]{:S(2)}, u32[]{:S(2)}) async-start(bf16[168,8,128]{2,0,1:T(8,128)(2,1)} %copy_bitcast_fusion.1), calls=%async_computation.1 | async-start | bytes 688128 | tf_op jit(solution)/shard_map/all_to_all | solution.py:106
  81.2 11.6 %all-to-all-done.1 = bf16[168,8,128]{2,0,1:T(8,128)(2,1)S(1)} async-done(((bf16[168,8,128]{2,0,1:T(8,128)(2,1)}), bf16[168,8,128]{2,0,1:T(8,128)(2,1)S(1)}, u32[]{:S(2)}, u32[]{:S(2)}) %all-to-all-start.1) | async-done | bytes 344096 | tf_op jit(solution)/shard_map/all_to_all | solution.py:106
  93.0 19.6 %all-gather.3.cloned.1.call-done = bf16[1344,2688]{1,0:T(8,128)(2,1)} async-done(((bf16[168,2688]{1,0:T(8,128)(2,1)}), bf16[1344,2688]{1,0:T(8,128)(2,1)}) %all-gather.3.cloned.1.call-update) | async-done | bytes 7225360 | tf_op jit(solution)/shard_map/all_gather | solution.py:42
  112.7 3.9 %fusion.2 = f32[128,1344]{0,1:T(8,128)S(1)} fusion(bf16[1344,128]{1,0:T(8,128)(2,1)S(1)} %get-tuple-element.12, bf16[1344,2688]{1,0:T(8,128)(2,1)} %all-gather.3.cloned.1.call-done), kind=kOutput, calls=%fused_computation.3 | convolution fusion | flops 462422016 | bytes 4816896 | tf_op jit(solution)/shard_map/dot_general | solution.py:123
  119.4 3.1 convolution_convert_fusion
  122.5 8.7 %convolution_convert_fusion.1 = bf16[1344,1344]{0,1:T(8,128)(2,1)} fusion(bf16[1344,128]{1,0:T(8,128)(2,1)S(1)} %get-tuple-element.12, f32[128,1344]{0,1:T(8,128)S(1)} %copy-done.8, bf16[128,1344]{0,1:T(8,128)(2,1)S(1)} %fusion.38, bf16[1344,2688]{1,0:T(8,128)(2,1)} %all-gather.3.cloned.1.call-done, f32[128,1344]{0,1:T(8,128)S(1)} %fusion.2), kind=kOutput, calls=%fused_computation.2 | convolution fusion | flops 928542720 | bytes 9461760 | tf_op jit(solution)/shard_map/dot_general | solution.py:136
  131.2 101.1 %fusion.75 = (bf16[96,1344]{1,0:T(8,128)(2,1)S(1)}, bf16[1344,96]{0,1:T(8,128)(2,1)S(1)}) fusion(bf16[1344,1344]{1,0:T(8,128)(2,1)} %convolution_convert_fusion, bf16[1344,1344]{0,1:T(8,128)(2,1)} %convolution_convert_fusion.1), kind=kCustom, calls=%all-reduce-scatter.2 | all-reduce-scatter fusion | flops 4128769 | bytes 7741952
  232.3 2.8 collective-permute-start
  236.5 4.2 %collective-permute-start.2 = (bf16[96,1344]{1,0:T(8,128)(2,1)S(1)}, bf16[96,1344]{1,0:T(8,128)(2,1)S(1)}, u32[]{:S(2)}, u32[]{:S(2)}) collective-permute-start(bf16[96,1344]{1,0:T(8,128)(2,1)S(1)} %get-tuple-element.4), channel_id=1, source_target_pairs={{0,1},{1,2},{2,3},{3,4},{4,5},{5,6},{6,7},{7,8},{8,9},{9,10},{10,1... | collective-permute-start | bytes 774152
  242.1 2.7 collective-permute-start.3
  245.2 3.1 concatenate.12
  248.9 7.4 %collective-permute-done.3 = bf16[84,1344]{1,0:T(8,128)(2,1)S(1)} collective-permute-done((bf16[84,1344]{1,0:T(8,128)(2,1)S(1)}, bf16[84,1344]{1,0:T(8,128)(2,1)S(1)}, u32[]{:S(2)}, u32[]{:S(2)}) %collective-permute-start.3) | collective-permute-done | bytes 225824
  256.3 3.1 concatenate.13
  261.6 29.3 %reduce-scatter.6.cloned.1.call-done = bf16[224,128]{1,0:T(8,128)(2,1)} async-done(((bf16[1792,128]{1,0:T(8,128)(2,1)}), bf16[224,128]{1,0:T(8,128)(2,1)}) %reduce-scatter.6.cloned.1.call-update) | async-done | bytes 57360 | tf_op jit(solution)/shard_map/reduce_scatter | solution.py:63
  292.3 8.6 %psum.30 = f32[168]{0:T(256)S(1)} all-reduce(f32[168]{0:T(256)S(1)} %fusion.62), channel_id=1, replica_groups=mesh['row'=8,'col_0'=4,'col_1'=4] {'col_0'}, use_global_device_ids=true, to_apply=%region_11.12 | all-reduce | flops 168 | bytes 1344 | tf_op jit(solution)/shard_map/psum | solution.py:34
  300.9 8.4 %psum.31 = f32[168]{0:T(256)S(1)} all-reduce(f32[168]{0:T(256)S(1)} %psum.30), channel_id=1, replica_groups=mesh['row'=8,'col_0'=4,'col_1'=4] {'col_1'}, use_global_device_ids=true, to_apply=%region_12.13 | all-reduce | flops 168 | bytes 1344 | tf_op jit(solution)/shard_map/psum | solution.py:34
  310.1 10.6 %all-to-all-start.3 = ((f32[8,1,84]{2,1,0:T(1,128)}), f32[8,1,84]{2,1,0:T(1,128)S(1)}, u32[]{:S(2)}, u32[]{:S(2)}) async-start(f32[8,1,84]{2,1,0:T(1,128)} %broadcast_in_dim.12), calls=%async_computation.4 | async-start | bytes 8192 | tf_op jit(solution)/shard_map/all_to_all | solution.py:24
  321.6 3.6 %all-to-all-done.3 = f32[8,1,84]{2,1,0:T(1,128)S(1)} async-done(((f32[8,1,84]{2,1,0:T(1,128)}), f32[8,1,84]{2,1,0:T(1,128)S(1)}, u32[]{:S(2)}, u32[]{:S(2)}) %all-to-all-start.3) | async-done | bytes 2720 | tf_op jit(solution)/shard_map/all_to_all | solution.py:24
  (78 shorter events, 21.5 us)
Async XLA Ops:
  7.2 62.3 %copy-start = (s32[64]{0:T(128)S(1)}, s32[64]{0:T(128)}, u32[]{:S(2)}) copy-start(s32[64]{0:T(128)} %param.8) | copy-start | bytes 772
  8.7 25.2 %all-to-all-start.2 = ((f32[8,1,84]{2,1,0:T(1,128)}), f32[8,1,84]{2,1,0:T(1,128)S(1)}, u32[]{:S(2)}, u32[]{:S(2)}) async-start(f32[8,1,84]{2,1,0:T(1,128)} %broadcast_in_dim.11), calls=%async_computation.2 | async-start | bytes 8192 | tf_op jit(solution)/shard_map/all_to_all | solution.py:24
  15.5 97.1 %all-gather.3.cloned.1.call-start = ((), (), s32[]{:S(2)}) async-start(), calls=%async_computation.5 | async-start | bytes 8128512 | tf_op jit(solution)/shard_map/all_gather | solution.py:42
  52.7 2.4 copy-start.2
  53.0 17.7 %copy-start.3 = (f32[168,1024]{1,0:T(8,128)S(1)}, f32[168,1024]{1,0:T(8,128)}, u32[]{:S(2)}) copy-start(f32[168,1024]{1,0:T(8,128)} %param.7) | copy-start | bytes 2064388
  55.9 20.7 %all-to-all-start = ((bf16[168,8,128]{2,0,1:T(8,128)(2,1)}), bf16[168,8,128]{2,0,1:T(8,128)(2,1)S(1)}, u32[]{:S(2)}, u32[]{:S(2)}) async-start(bf16[168,8,128]{2,0,1:T(8,128)(2,1)} %copy_bitcast_fusion.2), calls=%async_computation | async-start | bytes 688128 | tf_op jit(solution)/shard_map/all_to_all | solution.py:103
  76.6 16.2 %all-to-all-start.1 = ((bf16[168,8,128]{2,0,1:T(8,128)(2,1)}), bf16[168,8,128]{2,0,1:T(8,128)(2,1)S(1)}, u32[]{:S(2)}, u32[]{:S(2)}) async-start(bf16[168,8,128]{2,0,1:T(8,128)(2,1)} %copy_bitcast_fusion.1), calls=%async_computation.1 | async-start | bytes 688128 | tf_op jit(solution)/shard_map/all_to_all | solution.py:106
  81.1 35.4 %copy-start.7 = (f32[1,32,1344]{2,1,0:T(8,128)S(1)}, f32[1,32,1344]{2,1,0:T(8,128)}, u32[]{:S(2)}) copy-start(f32[1,32,1344]{2,1,0:T(8,128)} %param.9) | copy-start | bytes 516100
  81.1 209.7 %reduce-scatter.6.cloned.1.call-start = ((), (), s32[]{:S(2)}) async-start(), calls=%async_computation.6 | async-start | bytes 516096 | tf_op jit(solution)/shard_map/reduce_scatter | solution.py:63
  112.7 5.1 %copy-start.6 = (bf16[1344,2688]{1,0:T(8,128)(2,1)S(1)}, bf16[1344,2688]{1,0:T(8,128)(2,1)}, u32[]{:S(2)}) copy-start(bf16[1344,2688]{1,0:T(8,128)(2,1)} %all-gather.3.cloned.1.call-done) | copy-start | bytes 21676036
  119.4 3.1 copy-start.8
  131.2 109.6 %copy-start.5 = (u32[128]{0:T(128)S(1)}, u32[128]{0:T(128)}, u32[]{:S(2)}) copy-start(u32[128]{0:T(128)} %constant.95) | copy-start | bytes 1540
  232.3 12.9 %collective-permute-start = (bf16[1344,96]{0,1:T(8,128)(2,1)S(1)}, bf16[1344,96]{0,1:T(8,128)(2,1)S(1)}, u32[]{:S(2)}, u32[]{:S(2)}) collective-permute-start(bf16[1344,96]{0,1:T(8,128)(2,1)S(1)} %get-tuple-element.5), channel_id=1, source_target_pairs={{0,1},{1,2},{2,3},{3,4},{4,5},{5,6},{6,7},{7,8},{8,9},{9,10},{10,1... | collective-permute-start | bytes 774152
  235.2 10.0 %collective-permute-start.1 = (bf16[1344,84]{0,1:T(8,128)(2,1)S(1)}, bf16[1344,84]{0,1:T(8,128)(2,1)S(1)}, u32[]{:S(2)}, u32[]{:S(2)}) collective-permute-start(bf16[1344,84]{0,1:T(8,128)(2,1)S(1)} %slice.12), channel_id=1, source_target_pairs={{0,2},{1,3},{2,4},{3,5},{4,6},{5,7},{6,8},{7,9},{8,10},{9,11},{10,... | collective-permute-start | bytes 677384
  236.5 19.8 %collective-permute-start.2 = (bf16[96,1344]{1,0:T(8,128)(2,1)S(1)}, bf16[96,1344]{1,0:T(8,128)(2,1)S(1)}, u32[]{:S(2)}, u32[]{:S(2)}) collective-permute-start(bf16[96,1344]{1,0:T(8,128)(2,1)S(1)} %get-tuple-element.4), channel_id=1, source_target_pairs={{0,1},{1,2},{2,3},{3,4},{4,5},{5,6},{6,7},{7,8},{8,9},{9,10},{10,1... | collective-permute-start | bytes 774152
  242.1 14.2 %collective-permute-start.3 = (bf16[84,1344]{1,0:T(8,128)(2,1)S(1)}, bf16[84,1344]{1,0:T(8,128)(2,1)S(1)}, u32[]{:S(2)}, u32[]{:S(2)}) collective-permute-start(bf16[84,1344]{1,0:T(8,128)(2,1)S(1)} %slice.13), channel_id=1, source_target_pairs={{0,2},{1,3},{2,4},{3,5},{4,6},{5,7},{6,8},{7,9},{8,10},{9,11},{10,... | collective-permute-start | bytes 677384
  248.6 60.8 %copy-start.1 = (f32[1,168,84]{2,1,0:T(8,128)S(1)}, f32[1,168,84]{2,1,0:T(8,128)}, u32[]{:S(2)}) copy-start(f32[1,168,84]{2,1,0:T(8,128)} %param.10) | copy-start | bytes 169348
  248.9 71.8 %copy-start.4 = (f32[1,84,168]{2,0,1:T(1,128)S(1)}, f32[1,84,168]{2,0,1:T(1,128)}, u32[]{:S(2)}) copy-start(f32[1,84,168]{2,0,1:T(1,128)} %param.11) | copy-start | bytes 169348
  310.1 15.2 %all-to-all-start.3 = ((f32[8,1,84]{2,1,0:T(1,128)}), f32[8,1,84]{2,1,0:T(1,128)S(1)}, u32[]{:S(2)}, u32[]{:S(2)}) async-start(f32[8,1,84]{2,1,0:T(1,128)} %broadcast_in_dim.12), calls=%async_computation.4 | async-start | bytes 8192 | tf_op jit(solution)/shard_map/all_to_all | solution.py:24
Sparse Core Ops, SparseCore 0:
  55.2 57.3 all-gather.2
  261.7 29.0 reduce-scatter.5
where the time goes:
time: 334 us; the launch traced here: 333 us
  blocking collectives  153 us (46%)
  waiting for transfers between devices  77.1 us (23%)
  starting transfers between devices  46.5 us (14%)
  matrix products  18.5 us (6%)
  local copies, waits for them, and re-layouts  16.3 us (5%)
  between operations  15 us (4%)
  other arithmetic  6.88 us (2%)
    unnamed x1, blocking collectives  101 us
    psum x4, blocking collectives, one_axis_at_a_time(): value = lax.psum(value, axis)  34.1 us
    reduce_scatter x1, waiting for transfers between devices, sum_together(): lax.psum_scatter(lines, axis, tiled=True).reshape(-1)  29.3 us
    all_gather x1, waiting for transfers between devices, rows_first(): result = lax.all_gather(both, axis, axis=0, tiled=True)  19.6 us
    all_to_all x2, starting transfers between devices, sent_to_all(): return lax.all_to_all(copies, axis, split_axis=0, concat_axis=0, tiled=True)  17.4 us
    all_gather x1, blocking collectives, rows_first(): result = lax.all_gather(both, axis, axis=0, tiled=True)  17.3 us
    all_to_all x1, starting transfers between devices, local(): lax.all_to_all(clean.astype(jnp.bfloat16), 'row', split_axis=1, concat_ax...  13.5 us
    all_to_all x1, waiting for transfers between devices, local(): lax.all_to_all(noise.astype(jnp.bfloat16), 'row', split_axis=1, concat_ax...  11.6 us
  transfers between devices with their start and end apart: 10, of which 7 were waited for; matrix products, arithmetic and copies ran while one was open for 3% of the time, Pallas kernels for 0%

commit v1 on v0

v1 whole, which is shorter than its diff:
```python
import math

import jax
import jax.numpy as jnp
from jax import lax
from jax.experimental import pallas as pl
from jax.experimental.pallas import tpu as pltpu
from jax.sharding import PartitionSpec as P

MESH = pl.DeviceIdType.MESH
F32 = jnp.float32
BF16 = jnp.bfloat16

WIDTH = 1344
PIX = 256
SAMPLES = 64
BUCKETS = 32
MIX_WEIGHT = 0.3
KEEP_COEF = (1.0 - MIX_WEIGHT) / math.sqrt((1.0 - MIX_WEIGHT) ** 2 + MIX_WEIGHT**2)
ADD_COEF = MIX_WEIGHT / math.sqrt((1.0 - MIX_WEIGHT) ** 2 + MIX_WEIGHT**2)
SILU_GAIN = 1.0 / 0.596

ROWS = 8
CHAN = WIDTH // ROWS
CHAN_PAD = 176
CP = ROWS * CHAN_PAD
BLOCK = WIDTH // 16
HALF = BLOCK // 2
HP = 48
HT = 16 * HP
PACK = 384
NN = (((1,), (0,)), ((), ()))
NT = (((1,), (1,)), ((), ()))
TN = (((0,), (0,)), ((), ()))
MAX_COPIES = 160


def dot(a, b, dims):
    return lax.dot_general(a, b, dims, preferred_element_type=F32)


def kernel(
    clean, noise, bucket, mod, wz, out,
    st, tg, s_all, t_all, wz_in, wa, wb, ga, gb,
    ra1, ra2, rx1, rx2, rb1, rb2, ry1, ry2,
    gain, scale1, pre, hid, dpre, raw2, raw2_in, norm_row, norm_in,
    dbr, dbn, dh, zs, zr, send_sems, recv_sems,
):
    r = lax.axis_index("row")
    k = lax.axis_index("col")
    z, c = r // 2, r % 2
    y, x = k // 4, k % 4

    def peer(dz=0, dc=0, dy=0, dx=0):
        return (
            ((z + dz) % 4) * 2 + (c + dc) % 2,
            ((y + dy) % 4) * 4 + (x + dx) % 4,
        )

    started = []

    def send(src, dst, device):
        i = len(started)
        copy = pltpu.make_async_remote_copy(
            src_ref=src,
            dst_ref=dst,
            send_sem=send_sems.at[i],
            recv_sem=recv_sems.at[i],
            device_id=device,
            device_id_type=MESH,
        )
        copy.start()
        started.append(copy)
        return copy

    group = [(dz, dc) for dz in (2, 1, 3, 0) for dc in (0, 1) if (dz, dc) != (0, 0)]
    barrier = pltpu.get_barrier_semaphore()
    near = [peer(dz=dz, dc=dc) for dz, dc in group]
    near += [peer(dx=1), peer(dx=3), peer(dy=1), peer(dy=3)]
    for device in near:
        pl.semaphore_signal(barrier, inc=1, device_id=device, device_id_type=MESH)

    def state_piece(d):
        zq = (z + d) % 4
        level_of = jnp.full((1, PIX), bucket[k * 4 + zq], jnp.int32).astype(F32)
        level = jnp.exp(-3.0 + 5.0 * (level_of + 0.5) / BUCKETS)
        spread = jnp.sqrt(level * level + 0.25)
        cols = pl.ds(pl.multiple_of(zq * PIX, PIX), PIX)
        cl = clean[:, cols]
        no = noise[:, cols]
        pad = jnp.zeros((CHAN_PAD - CHAN, PIX), F32)
        state = (cl + level * no) / spread
        target = cl * (2.0 * level / spread) - no * (0.5 / spread)
        return (
            jnp.concatenate([state, pad], axis=0).astype(BF16),
            jnp.concatenate([target, pad], axis=0).astype(BF16),
        )

    for d in range(4):
        state, target = state_piece(d)
        st[d] = state
        tg[d] = target
    s_all[r] = st[0]
    t_all[r] = tg[0]
    wz_in[r] = wz[c]

    pl.semaphore_wait(barrier, len(near))

    w_copies = [
        send(wz.at[(c + dc) % 2], wz_in.at[r], peer(dz=dz, dc=dc)) for dz, dc in group
    ]
    s_copies = {d: send(st.at[d], s_all.at[r], peer(dz=d)) for d in (2, 1, 3)}
    s_own = send(st.at[0], s_all.at[r], peer(dc=1))
    t_copies = {d: send(tg.at[d], t_all.at[r], peer(dz=d)) for d in (2, 1, 3)}
    t_own = send(tg.at[0], t_all.at[r], peer(dc=1))

    sample = k * 4 + z
    picked = lax.broadcasted_iota(jnp.int32, (BUCKETS, CP), 0) == bucket[sample]
    mod_row = jnp.sum(jnp.where(picked, 1.0 + mod[...], 0.0), axis=0, keepdims=True)
    for b in range(16):
        first = (BLOCK * b // 128) * 128
        lane = lax.broadcasted_iota(jnp.int32, (HP, 256), 1) + first
        row = lax.broadcasted_iota(jnp.int32, (HP, 256), 0)
        take = (lane == row + (BLOCK * b + HALF * c)) & (row < HALF)
        window = jnp.broadcast_to(mod_row[:, first : first + 256], (HP, 256))
        value = jnp.sum(jnp.where(take, window, 0.0), axis=1, keepdims=True)
        gain[b] = jnp.broadcast_to(value, (HP, PIX))

    for copy in w_copies:
        copy.wait_recv()
    wa[y, x] = jnp.concatenate(
        [wz_in[q][:, :CHAN_PAD].astype(F32) for q in range(ROWS)], axis=1
    ).astype(BF16)
    wb[x, y] = jnp.concatenate(
        [wz_in[q][:, CHAN_PAD : 2 * CHAN_PAD].astype(F32) for q in range(ROWS)], axis=1
    ).astype(BF16)

    class Side:
        pass

    def side_a():
        s = Side()
        s.w, s.g, s.i1, s.i2 = wa, ga, x, y
        s.p1 = lambda d: peer(dx=d)
        s.p2 = lambda d: peer(dy=d)
        s.cut = 32
        s.half1, s.half2, s.full1, s.full2 = rx1, ra1, rx2, ra2
        return s

    def side_b():
        s = Side()
        s.w, s.g, s.i1, s.i2 = wb, gb, y, x
        s.p1 = lambda d: peer(dy=d)
        s.p2 = lambda d: peer(dx=d)
        s.cut = 16
        s.half1, s.half2, s.full1, s.full2 = ry1, rb1, ry2, rb2
        return s

    a, b = side_a(), side_b()

    def at1(s, d):
        return (s.i1 + d) % 4

    def at2(s, d):
        return (s.i2 + d) % 4

    def own_out(s):
        block = s.w.at[s.i2, s.i1]
        s.first = {d: send(block, block, s.p1(d)) for d in (1, 3)}

    def spread_out(s, d):
        block = s.w.at[s.i2, at1(s, d)]
        s.second[d] = {e: send(block, block, s.p2(e)) for e in (1, 3)}

    for s in (a, b):
        own_out(s)
    for s in (a, b):
        s.second = {}
        spread_out(s, 0)

    for s in (a, b):
        s.first[1].wait_recv()
        block = s.w.at[s.i2, at1(s, 3), pl.ds(0, s.cut)]
        s.far_up = send(block, block, s.p1(1))
        s.first[3].wait_recv()
        block = s.w.at[s.i2, at1(s, 1), pl.ds(s.cut, HP - s.cut)]
        s.far_down = send(block, block, s.p1(3))
        spread_out(s, 3)
        spread_out(s, 1)
    for d in (2, 1, 3):
        s_copies[d].wait_recv()
        slot = s_all.at[((z - d) % 4) * 2 + c]
        s_copies[d + 4] = send(slot, slot, peer(dc=1))
    for s in (a, b):
        s.far_up.wait_recv()
        s.far_down.wait_recv()
        spread_out(s, 2)
    s_own.wait_recv()
    for s in (a, b):
        s.far = {}
        for d in (0, 3):
            s.second[d][1].wait_recv()
            block = s.w.at[at2(s, 3), at1(s, d)]
            s.far[d] = send(block, block, s.p2(1))
        for d in (1, 2):
            s.second[d][3].wait_recv()
            block = s.w.at[at2(s, 1), at1(s, d)]
            s.far[d] = send(block, block, s.p2(3))
    for d in (2, 1, 3):
        t_copies[d].wait_recv()
        slot = t_all.at[((z - d) % 4) * 2 + c]
        t_copies[d + 4] = send(slot, slot, peer(dc=1))
        s_copies[d + 4].wait_recv()
    t_own.wait_recv()
    for s in (a, b):
        for d in (0, 3):
            s.second[d][3].wait_recv()
        for d in (1, 2):
            s.second[d][1].wait_recv()
        for d in range(4):
            s.far[d].wait_recv()

    def square_rows(i, total):
        block = wb[i // 4, i % 4].astype(F32)
        return total + jnp.sum((block * block).reshape(HP // 8, 8, CP), axis=0)

    norm_row[0] = lax.fori_loop(0, 16, square_rows, jnp.zeros((8, CP), F32))
    n_copy = send(norm_row.at[0], norm_in, peer(dc=1))

    def first_matmul(i, _):
        slab = wa[i].reshape(4 * HP, CP)
        pre[pl.ds(i * 4, 4)] = dot(slab, s_all[...].reshape(CP, PIX), NN).reshape(4, HP, PIX)
        return 0

    lax.fori_loop(0, 4, first_matmul, 0)

    def activate(i, _):
        block = wa[i // 4, i % 4].astype(F32)
        squares = jnp.sum(block * block, axis=1, keepdims=True)
        inv = jnp.broadcast_to(lax.rsqrt(squares + 1.0), (HP, PIX))
        value = pre[i] * inv
        pre[i] = value
        hidden = value * jax.nn.sigmoid(value) * SILU_GAIN * gain[i]
        hid[(i % 4) * 4 + i // 4] = hidden.astype(BF16)
        return 0

    lax.fori_loop(0, 16, activate, 0)

    def second_matmul(i, _):
        for part in range(2):
            cols = slice(part * 768, min(CP, (part + 1) * 768))
            value = dot(
                wb[i, :, :, cols].reshape(4 * HP, -1), hid[pl.ds(i * 4, 4)].reshape(4 * HP, PIX), TN
            )
            @pl.when(i == 0)
            def _():
                raw2[cols, :] = value
            @pl.when(i > 0)
            def _():
                raw2[cols, :] += value
        return 0

    lax.fori_loop(0, 4, second_matmul, 0)
    raw_copy = send(raw2, raw2_in, peer(dc=1))

    n_copy.wait_recv()
    norm = jnp.sum(norm_row[0] + norm_in[...], axis=0, keepdims=True)
    inv_row = lax.rsqrt(norm + 1.0)
    norm_row[1] = jnp.broadcast_to(inv_row, (8, CP))
    raw_copy.wait_recv()
    for d in (2, 1, 3):
        t_copies[d + 4].wait_recv()

    dot_row = jnp.zeros((16, CP), F32)
    for q in range(CP // 128):
        rows = pl.ds(q * 128, 128)
        inv_col = jnp.broadcast_to(inv_row[:, q * 128 : (q + 1) * 128], (128, 128)).T
        inv_col = jnp.concatenate([inv_col, inv_col], axis=1)
        total = raw2[rows, :] + raw2_in[rows, :]
        state = s_all[...].reshape(CP, PIX)[q * 128 : (q + 1) * 128].astype(F32)
        target = t_all[...].reshape(CP, PIX)[q * 128 : (q + 1) * 128].astype(F32)
        grad = (KEEP_COEF * state + ADD_COEF * (total * inv_col) - target) / SAMPLES
        dbranch = (ADD_COEF * grad).astype(BF16)
        dbr[rows, :] = dbranch
        wide = dbranch.astype(F32)
        dbn[rows, :] = (wide * inv_col).astype(BF16)
        raw2_in[rows, :] = wide * total
    dot_row = dot(jnp.ones((16, PIX), BF16), raw2_in[...].astype(BF16), NT)[0:1]
    dot_high = dot_row.astype(BF16).astype(F32)
    dot_low = dot_row - dot_high

    row = lax.broadcasted_iota(jnp.int32, (HP, 1), 0)

    def second_grad(i, _):
        value = dot(hid[pl.ds(i * 4, 4)].reshape(4 * HP, PIX), dbr[...], NT)
        for j in range(4):
            block = value[j * HP : (j + 1) * HP]
            block = jnp.where(row == HALF, dot_high, block)
            block = jnp.where(row == HALF + 1, dot_low, block)
            gb[i, j] = block.astype(BF16)
        return 0

    def first_grad(i, _):
        value = dot(dpre[pl.ds(i * 4, 4)].reshape(4 * HP, PIX), s_all[...].reshape(CP, PIX), NT)
        ga[i] = value.reshape(4, HP, CP).astype(BF16)
        return 0

    def hidden_grad(i, _):
        dh[pl.ds(i * 4, 4)] = dot(wb[i].reshape(4 * HP, CP), dbn[...], NN).reshape(4, HP, PIX)
        return 0

    def activate_grad(i, _):
        value = pre[i]
        sig = jax.nn.sigmoid(value)
        slope = sig * (1.0 + value * (1.0 - sig))
        grad = dh[(i % 4) * 4 + i // 4]
        dpre[i] = (grad * gain[i] * slope * SILU_GAIN).astype(BF16)
        return 0

    def scatter_far(s):
        s.got_half = {}
        for n, d in enumerate((0, 1)):
            s.got_half[d] = send(s.g.at[at2(s, 2), at1(s, d)], s.half2.at[n], s.p2(1))
        for n, d in enumerate((2, 3)):
            s.got_half[d] = send(s.g.at[at2(s, 2), at1(s, d)], s.half2.at[2 + n], s.p2(3))

    def scatter_near(s):
        s.got_full = {}
        for d in (2, 3):
            s.got_full[0, d] = send(s.g.at[at2(s, 1), at1(s, d)], s.full2.at[0, d], s.p2(1))
        for d in (0, 1):
            s.got_full[1, d] = send(s.g.at[at2(s, 3), at1(s, d)], s.full2.at[1, d], s.p2(3))

    def scatter_relay(s):
        for n, d in enumerate((0, 1, 2, 3)):
            s.got_half[d].wait_recv()
            up = d < 2
            spot = (at2(s, 1 if up else 3), at1(s, d))
            s.g[spot] = (s.g[spot].astype(F32) + s.half2[n].astype(F32)).astype(BF16)
            way = 0 if up else 1
            s.got_full[way, d] = send(
                s.g.at[spot[0], spot[1]], s.full2.at[way, d], s.p2(1 if up else 3)
            )

    def scatter_sum(s, d):
        s.got_full[0, d].wait_recv()
        s.got_full[1, d].wait_recv()
        spot = (s.i2, at1(s, d))
        total = (
            s.g[spot].astype(F32) + s.full2[0, d].astype(F32) + s.full2[1, d].astype(F32)
        )
        if d == 0:
            s.own = total
        s.g[spot] = total.astype(BF16)

    def ring_far(s):
        spot = s.g.at[s.i2, at1(s, 2)]
        low, high = pl.ds(0, s.cut), pl.ds(s.cut, HP - s.cut)
        s.far_up = send(spot.at[low], s.half1.at[low], s.p1(1))
        s.far_down = send(spot.at[high], s.half1.at[high], s.p1(3))

    def ring_near(s):
        low, high = pl.ds(0, s.cut), pl.ds(s.cut, HP - s.cut)
        s.near = [
            send(s.g.at[s.i2, at1(s, 1), high], s.full1.at[0, high], s.p1(1)),
            send(s.g.at[s.i2, at1(s, 3), low], s.full1.at[1, low], s.p1(3)),
        ]

    def ring_relay(s):
        low, high = slice(0, s.cut), slice(s.cut, HP)
        for copy, part, d, way in ((s.far_up, low, 1, 0), (s.far_down, high, 3, 1)):
            copy.wait_recv()
            at = at1(s, d)
            s.g[s.i2, at, part] = (
                s.g[s.i2, at, part].astype(F32) + s.half1[part].astype(F32)
            ).astype(BF16)
            rows = pl.ds(part.start, part.stop - part.start)
            s.near.append(send(s.g.at[s.i2, at, rows], s.full1.at[way, rows], s.p1(d)))

    def ring_sum(s):
        for copy in s.near:
            copy.wait_recv()
        return s.own + s.full1[0].astype(F32) + s.full1[1].astype(F32)

    lax.fori_loop(0, 4, second_grad, 0)
    scatter_far(b)
    scatter_near(b)
    lax.fori_loop(0, 4, hidden_grad, 0)
    lax.fori_loop(0, 16, activate_grad, 0)
    lax.fori_loop(0, 4, first_grad, 0)
    scatter_far(a)
    scatter_near(a)
    scatter_relay(b)
    scatter_relay(a)
    for s in (b, a):
        scatter_sum(s, 2)
        ring_far(s)
        scatter_sum(s, 1)
        scatter_sum(s, 3)
        ring_near(s)
        scatter_sum(s, 0)
    ring_relay(b)
    ring_relay(a)
    grad2 = ring_sum(b)
    grad1 = ring_sum(a)

    w1 = wa[y, x].astype(F32)
    inv1 = lax.rsqrt(jnp.sum(w1 * w1, axis=1, keepdims=True) + 1.0)
    dot1 = jnp.sum(w1 * grad1, axis=1, keepdims=True)
    out1 = grad1 * inv1 - w1 * (dot1 * inv1 * inv1 * inv1)
    w2 = wb[x, y].astype(F32)
    inv2 = norm_row[1][0:1]
    dot2 = grad2[HALF : HALF + 1] + grad2[HALF + 1 : HALF + 2]
    out2 = grad2 * inv2 - w2 * (dot2 * inv2 * inv2 * inv2)
    fill = jnp.zeros((HP, PACK - 2 * CHAN_PAD), F32)
    for q in range(ROWS):
        cols = slice(q * CHAN_PAD, (q + 1) * CHAN_PAD)
        zs[q] = jnp.concatenate([out1[:, cols], out2[:, cols], fill], axis=1).astype(BF16)
    z_copies = [
        send(zs.at[((z + dz) % 4) * 2 + (c + dc) % 2], zr.at[r], peer(dz=dz, dc=dc))
        for dz, dc in group
    ]
    zr[r] = zs[r]
    for copy in z_copies:
        copy.wait_recv()
    for core in range(2):
        out[core] = sum(zr[2 * q + core].astype(F32) for q in range(4))
    for copy in started:
        copy.wait_send()


def local(clean, noise, bucket, mod_table, w_first, w_second):
    def halves(w):
        w = w.reshape(2, HALF, CHAN)
        return jnp.pad(w, ((0, 0), (0, HP - HALF), (0, CHAN_PAD - CHAN)))

    packed = jnp.concatenate([halves(w_first[0].T), halves(w_second[0])], axis=2)
    packed = jnp.pad(packed, ((0, 0), (0, 0), (0, PACK - 2 * CHAN_PAD))).astype(BF16)
    mod = jnp.pad(mod_table[0], ((0, 0), (0, CP - WIDTH)))
    vmem = pl.BlockSpec(memory_space=pltpu.VMEM)
    smem = pl.BlockSpec(memory_space=pltpu.SMEM)
    block = (HP, CP)
    result = pl.pallas_call(
        kernel,
        out_shape=jax.ShapeDtypeStruct((2, HP, PACK), F32),
        in_specs=[vmem, vmem, smem, vmem, vmem],
        out_specs=vmem,
        scratch_shapes=[
            pltpu.VMEM((4, CHAN_PAD, PIX), BF16),
            pltpu.VMEM((4, CHAN_PAD, PIX), BF16),
            pltpu.VMEM((ROWS, CHAN_PAD, PIX), BF16),
            pltpu.VMEM((ROWS, CHAN_PAD, PIX), BF16),
            pltpu.VMEM((ROWS, HP, PACK), BF16),
            pltpu.VMEM((4, 4, *block), BF16),
            pltpu.VMEM((4, 4, *block), BF16),
            pltpu.VMEM((4, 4, *block), BF16),
            pltpu.VMEM((4, 4, *block), BF16),
            pltpu.VMEM((4, *block), BF16),
            pltpu.VMEM((2, 4, *block), BF16),
            pltpu.VMEM(block, BF16),
            pltpu.VMEM((2, *block), BF16),
            pltpu.VMEM((4, *block), BF16),
            pltpu.VMEM((2, 4, *block), BF16),
            pltpu.VMEM(block, BF16),
            pltpu.VMEM((2, *block), BF16),
            pltpu.VMEM((16, HP, PIX), F32),
            pltpu.VMEM((16, HP, PIX), F32),
            pltpu.VMEM((16, HP, PIX), F32),
            pltpu.VMEM((16, HP, PIX), BF16),
            pltpu.VMEM((16, HP, PIX), BF16),
            pltpu.VMEM((CP, PIX), F32),
            pltpu.VMEM((CP, PIX), F32),
            pltpu.VMEM((2, 8, CP), F32),
            pltpu.VMEM((8, CP), F32),
            pltpu.VMEM((CP, PIX), BF16),
            pltpu.VMEM((CP, PIX), BF16),
            pltpu.VMEM((16, HP, PIX), F32),
            pltpu.VMEM((ROWS, HP, PACK), BF16),
            pltpu.VMEM((ROWS, HP, PACK), BF16),
            pltpu.SemaphoreType.DMA((MAX_COPIES,)),
            pltpu.SemaphoreType.DMA((MAX_COPIES,)),
        ],
        compiler_params=pltpu.CompilerParams(
            collective_id=0, has_side_effects=True, vmem_limit_bytes=60 * 1024 * 1024
        ),
    )(clean, noise, bucket, mod, packed)
    part = result[:, :HALF]
    first = part[:, :, :CHAN].reshape(BLOCK, CHAN).T
    second = part[:, :, CHAN_PAD : CHAN_PAD + CHAN].reshape(BLOCK, CHAN)
    return first[None], second[None]


def solution(mesh):
    in_specs = (
        P("row", "col"),
        P("row", "col"),
        P(),
        P(),
        P(None, "row", "col"),
        P(None, "col", "row"),
    )
    out_specs = (P(None, "row", "col"), P(None, "col", "row"))
    return jax.shard_map(local, mesh=mesh, in_specs=in_specs, out_specs=out_specs, check_vma=False)
```

time: 334 us -> 99.4 us (0.30)
  blocking collectives: 153 us -> 0 us
  Pallas kernels: 0 us -> 92.3 us
  waiting for transfers between devices: 77.1 us -> 0 us
  starting transfers between devices: 46.5 us -> 0 us
  matrix products: 18.5 us -> 0 us
  between operations: 15 us -> 0.67 us
  local copies, waits for them, and re-layouts: 16.3 us -> 4.96 us
  other arithmetic: 6.88 us -> 1.21 us
    unnamed x1 -> x0, blocking collectives: 101 us -> none
    pallas_call x0 -> x1, Pallas kernels: none -> 92.3 us  [local(): pl.pallas_call(kernel, out_shape=jax.ShapeDtypeStruct((2, HP, PACK), F32)...]
    all_to_all x4 -> x0, starting transfers between devices: 35.4 us -> none  [the longest x2 17.4 us: sent_to_all(): return lax.all_to_all(copies, axis, split_axis=0, concat_axis=0, tiled=True)]
    psum x4 -> x0, blocking collectives: 34.1 us -> none  [one_axis_at_a_time(): value = lax.psum(value, axis)]
    reduce_scatter x1 -> x0, waiting for transfers between devices: 29.3 us -> none  [sum_together(): lax.psum_scatter(lines, axis, tiled=True).reshape(-1)]
    all_to_all x4 -> x0, waiting for transfers between devices: 20.4 us -> none  [the longest x1 11.6 us: local(): lax.all_to_all(noise.astype(jnp.bfloat16), 'row', split_axis=1, concat_ax...]
    all_gather x1 -> x0, waiting for transfers between devices: 19.6 us -> none  [rows_first(): result = lax.all_gather(both, axis, axis=0, tiled=True)]
    dot_general x5 -> x0, matrix products: 18.5 us -> none  [the longest x1 8.72 us: local(): lax.dot_general(state_own, dpre, CONTRACT_LEAD, preferred_element_type=jn...]
  transfers between devices with their start and end apart: 10 -> 0, of which waited for: 7 -> 0; matrix products, arithmetic and copies ran while one was open for 3% -> 0% of each run, Pallas kernels for 0% -> 0%
where the time goes in v1:
time: 99.4 us; the launch traced here: 99.2 us
  Pallas kernels  92.3 us (93%)
  local copies, waits for them, and re-layouts  4.96 us (5%)
  other arithmetic  1.21 us (1%)
    pallas_call x1, Pallas kernels, local(): pl.pallas_call(kernel, out_shape=jax.ShapeDtypeStruct((2, HP, PACK), F32)...  92.3 us

profile of v1, /device:TPU:1, one launch (start us, length us, event | category | flops | bytes accessed | tf_op | source)
XLA Modules:
  0.0 99.2 jit_solution(3471500193632227397)
XLA Ops:
  0.6 0.9 convert_bitcast_fusion
  1.5 0.0 copy-start.1
  1.5 0.1 copy.11
  1.7 0.7 copy-done.1
  2.4 0.2 convert_reduce_fusion
  2.7 0.0 copy-start
  2.7 0.1 fusion.2
  2.8 0.6 pad.21.wz
  3.4 0.2 copy-done
  3.6 0.7 pad.18.mod
  4.3 92.3 %shard_map.77 = f32[2,48,384]{2,1,0:T(8,128)} custom-call(f32[168,1024]{1,0:T(8,128)} %clean.1, f32[168,1024]{1,0:T(8,128)} %noise.1, s32[64]{0:T(128)} %bucket.1, f32[32,1408]{1,0:T(8,128)} %pad.18.mod, bf16[2,48,384]{2,1,0:T(8,128)(2,1)} %pad.21.wz), custom_call_target="tpu_custom_call" | custom-call | tf_op jit(solution)/shard_map/pallas_call | solution.py:443
  96.6 1.1 %fusion.3 = (f32[2,42,168]{2,1,0:T(8,128)S(1)}, f32[2,42,168]{2,1,0:T(8,128)S(1)}) fusion(f32[2,48,384]{2,1,0:T(8,128)} %shard_map.77), kind=kLoop, calls=%fused_computation.7 | loop fusion | bytes 225792 | tf_op jit(solution)/shard_map/slice | solution.py:489
  97.7 0.7 broadcast_in_dim_reshape.4
  98.4 0.7 copy.12
  (3 shorter events, 0.1 us)
Async XLA Ops:
  1.5 0.9 copy-start.1
  2.7 0.9 copy-start

commit v2 on v1

v2 whole, which is shorter than its diff:
```python
import math

import jax
import jax.numpy as jnp
from jax import lax
from jax.experimental import pallas as pl
from jax.experimental.pallas import tpu as pltpu
from jax.sharding import PartitionSpec as P

MESH = pl.DeviceIdType.MESH
F32 = jnp.float32
BF16 = jnp.bfloat16

WIDTH = 1344
PIX = 256
SAMPLES = 64
BUCKETS = 32
MIX_WEIGHT = 0.3
KEEP_COEF = (1.0 - MIX_WEIGHT) / math.sqrt((1.0 - MIX_WEIGHT) ** 2 + MIX_WEIGHT**2)
ADD_COEF = MIX_WEIGHT / math.sqrt((1.0 - MIX_WEIGHT) ** 2 + MIX_WEIGHT**2)
SILU_GAIN = 1.0 / 0.596

ROWS = 8
CHAN = WIDTH // ROWS
CHAN_PAD = 176
CP = ROWS * CHAN_PAD
BLOCK = WIDTH // 16
HALF = BLOCK // 2
HP = 48
HT = 16 * HP
WP = 256
CUTS = ((0, 768), (768, 1408))
NN = (((1,), (0,)), ((), ()))
NT = (((1,), (1,)), ((), ()))
TN = (((0,), (0,)), ((), ()))
MAX_COPIES = 160


def dot(a, b, dims):
    return lax.dot_general(a, b, dims, preferred_element_type=F32)


def kernel(
    clean_hbm, noise_hbm, bucket, mod_hbm, w1_hbm, w2_hbm, out1, out2,
    clean, noise, mod, w1_in, w2_in, w1_out, w2_out, w1_got, w2_got,
    st, tg, s_all, t_all, s_tok, t_tok, wa, wb, ga, gb,
    ra1, ra2, rx1, rx2, rb1, rb2, ry1, ry2,
    gain, pre, hid, dpre, raw, raw_out, raw_in, norm_row, norm_in,
    dbr, dbn, dot_rows, dh, zs1, zs2, zr1, zr2, load_sems, send_sems, recv_sems,
):
    r = lax.axis_index("row")
    k = lax.axis_index("col")
    z, c = r // 2, r % 2
    y, x = k // 4, k % 4

    def peer(dz=0, dc=0, dy=0, dx=0):
        return (
            ((z + dz) % 4) * 2 + (c + dc) % 2,
            ((y + dy) % 4) * 4 + (x + dx) % 4,
        )

    started = []

    def send(src, dst, device):
        i = len(started)
        copy = pltpu.make_async_remote_copy(
            src_ref=src,
            dst_ref=dst,
            send_sem=send_sems.at[i],
            recv_sem=recv_sems.at[i],
            device_id=device,
            device_id_type=MESH,
        )
        copy.start()
        started.append(copy)
        return copy

    group = [(dz, dc) for dz in (1, 3, 2, 0) for dc in (0, 1) if (dz, dc) != (0, 0)]
    barrier = pltpu.get_barrier_semaphore()
    near = [peer(dz=dz, dc=dc) for dz, dc in group]
    near += [peer(dx=1), peer(dx=3), peer(dy=1), peer(dy=3)]
    for device in near:
        pl.semaphore_signal(barrier, inc=1, device_id=device, device_id_type=MESH)

    loads = [
        pltpu.make_async_copy(src, dst, load_sems.at[i])
        for i, (src, dst) in enumerate(
            (
                (w1_hbm.at[0], w1_in),
                (w2_hbm.at[0], w2_in),
                (clean_hbm, clean),
                (noise_hbm, noise),
                (mod_hbm.at[0], mod),
            )
        )
    ]
    for load in loads:
        load.start()

    loads[0].wait()
    loads[1].wait()
    hid_of = lax.broadcasted_iota(jnp.int32, (HP, BLOCK), 0)
    col_of = lax.broadcasted_iota(jnp.int32, (HP, BLOCK), 1)
    w1_bf = w1_in[...].astype(BF16)
    w2_bf = w2_in[...].astype(BF16)
    for core in range(2):
        pick = (col_of == hid_of + HALF * core) & (hid_of < HALF)
        pick = jnp.where(pick, 1.0, 0.0).astype(BF16)
        fill = jnp.zeros((HP, WP - CHAN), F32)
        w1_out[core] = jnp.concatenate([dot(pick, w1_bf, NT), fill], axis=1).astype(BF16)
        w2_out[core] = jnp.concatenate([dot(pick, w2_bf, NN), fill], axis=1).astype(BF16)
    w1_got[r] = w1_out[c]
    w2_got[r] = w2_out[c]

    def state_piece(d):
        zq = (z + d) % 4
        level_of = jnp.full((1, PIX), bucket[k * 4 + zq], jnp.int32).astype(F32)
        level = jnp.exp(-3.0 + 5.0 * (level_of + 0.5) / BUCKETS)
        spread = jnp.sqrt(level * level + 0.25)
        cols = pl.ds(pl.multiple_of(zq * PIX, PIX), PIX)
        cl = clean[:, cols]
        no = noise[:, cols]
        pad = jnp.zeros((CHAN_PAD - CHAN, PIX), F32)
        state = (cl + level * no) / spread
        target = cl * (2.0 * level / spread) - no * (0.5 / spread)
        return (
            jnp.concatenate([state, pad], axis=0).astype(BF16),
            jnp.concatenate([target, pad], axis=0).astype(BF16),
        )

    loads[2].wait()
    loads[3].wait()
    loads[4].wait()
    for d in range(4):
        state, target = state_piece(d)
        st[d] = state
        tg[d] = target
    s_all[r] = st[0]
    t_all[r] = tg[0]

    pl.semaphore_wait(barrier, len(near))

    w1_copies = [
        send(w1_out.at[(c + dc) % 2], w1_got.at[r], peer(dz=dz, dc=dc)) for dz, dc in group
    ]
    w2_copies = [
        send(w2_out.at[(c + dc) % 2], w2_got.at[r], peer(dz=dz, dc=dc)) for dz, dc in group
    ]
    s_copies = {d: send(st.at[d], s_all.at[r], peer(dz=d)) for d in (2, 1, 3)}
    s_own = send(st.at[0], s_all.at[r], peer(dc=1))
    t_copies = {d: send(tg.at[d], t_all.at[r], peer(dz=d)) for d in (2, 1, 3)}
    t_own = send(tg.at[0], t_all.at[r], peer(dc=1))

    sample = k * 4 + z
    picked = lax.broadcasted_iota(jnp.int32, (BUCKETS, WIDTH), 0) == bucket[sample]
    mod_row = jnp.sum(jnp.where(picked, 1.0 + mod[...], 0.0), axis=0, keepdims=True)
    mod_row = jnp.concatenate([mod_row, jnp.zeros((1, CP - WIDTH), F32)], axis=1)
    for b in range(16):
        first = (BLOCK * b // 128) * 128
        lane = lax.broadcasted_iota(jnp.int32, (HP, 256), 1) + first
        row = lax.broadcasted_iota(jnp.int32, (HP, 256), 0)
        take = (lane == row + (BLOCK * b + HALF * c)) & (row < HALF)
        window = jnp.broadcast_to(mod_row[:, first : first + 256], (HP, 256))
        value = jnp.sum(jnp.where(take, window, 0.0), axis=1, keepdims=True)
        gain[b] = jnp.broadcast_to(value, (HP, PIX))

    class Side:
        pass

    def side_a():
        s = Side()
        s.w, s.g, s.i1, s.i2 = wa, ga, x, y
        s.p1 = lambda d: peer(dx=d)
        s.p2 = lambda d: peer(dy=d)
        s.cut = 32
        s.half1, s.half2, s.full1, s.full2 = rx1, ra1, rx2, ra2
        return s

    def side_b():
        s = Side()
        s.w, s.g, s.i1, s.i2 = wb, gb, y, x
        s.p1 = lambda d: peer(dy=d)
        s.p2 = lambda d: peer(dx=d)
        s.cut = 16
        s.half1, s.half2, s.full1, s.full2 = ry1, rb1, ry2, rb2
        return s

    a, b = side_a(), side_b()

    def at1(s, d):
        return (s.i1 + d) % 4

    def at2(s, d):
        return (s.i2 + d) % 4

    def spread_out(s, d):
        block = s.w.at[s.i2, at1(s, d)]
        s.second[d] = {e: send(block, block, s.p2(e)) for e in (1, 3)}

    for s, copies, got in ((a, w1_copies, w1_got), (b, w2_copies, w2_got)):
        for copy in copies:
            copy.wait_recv()
        s.w[s.i2, s.i1] = jnp.concatenate(
            [got[q][:, :CHAN_PAD].astype(F32) for q in range(ROWS)], axis=1
        ).astype(BF16)
        block = s.w.at[s.i2, s.i1]
        s.first = {d: send(block, block, s.p1(d)) for d in (1, 3)}
        s.second = {}
        spread_out(s, 0)

    for s in (a, b):
        s.first[1].wait_recv()
        block = s.w.at[s.i2, at1(s, 3), pl.ds(0, s.cut)]
        s.far_up = send(block, block, s.p1(1))
        s.first[3].wait_recv()
        block = s.w.at[s.i2, at1(s, 1), pl.ds(s.cut, HP - s.cut)]
        s.far_down = send(block, block, s.p1(3))
        spread_out(s, 3)
        spread_out(s, 1)
    for d in (2, 1, 3):
        s_copies[d].wait_recv()
        slot = s_all.at[((z - d) % 4) * 2 + c]
        s_copies[d + 4] = send(slot, slot, peer(dc=1))
    for s in (a, b):
        s.far_up.wait_recv()
        s.far_down.wait_recv()
        spread_out(s, 2)
        s.far = {}
    s_own.wait_recv()
    for d in (2, 1, 3):
        s_copies[d + 4].wait_recv()

    def first_half(slab):
        weights = wa[slab].reshape(4 * HP, CP)
        value = dot(weights, s_all[...].reshape(CP, PIX), NN).reshape(4, HP, PIX)
        for j in range(4):
            block = wa[slab, j].astype(F32)
            squares = jnp.sum(block * block, axis=1, keepdims=True)
            inv = jnp.broadcast_to(lax.rsqrt(squares + 1.0), (HP, PIX))
            act = value[j] * inv
            pre[slab * 4 + j] = act
            hidden = act * jax.nn.sigmoid(act) * SILU_GAIN * gain[slab * 4 + j]
            hid[j * 4 + slab] = hidden.astype(BF16)

    first_half(y)
    s_tok[...] = s_all[...].reshape(CP, PIX).T

    def pass_on(s, d, up):
        if up:
            s.second[d][1].wait_recv()
            block = s.w.at[at2(s, 3), at1(s, d)]
            s.far[d] = send(block, block, s.p2(1))
        else:
            s.second[d][3].wait_recv()
            block = s.w.at[at2(s, 1), at1(s, d)]
            s.far[d] = send(block, block, s.p2(3))

    for d, up in ((0, True), (3, False), (1, True), (2, False)):
        pass_on(a, d, up)
        pass_on(b, d, up)
    for d in (2, 1, 3):
        t_copies[d].wait_recv()
        slot = t_all.at[((z - d) % 4) * 2 + c]
        t_copies[d + 4] = send(slot, slot, peer(dc=1))

    def squares_of(slab):
        total = jnp.zeros((8, CP), F32)
        for j in range(4):
            block = wb[slab, j].astype(F32)
            total = total + jnp.sum((block * block).reshape(HP // 8, 8, CP), axis=0)
        return total

    for d in (3, 2):
        a.second[d][1].wait_recv()
    first_half(at2(a, 3))
    for d in (0, 1):
        a.second[d][3].wait_recv()
    first_half(at2(a, 1))
    t_own.wait_recv()
    for d in (2, 1, 3):
        t_copies[d + 4].wait_recv()
    t_tok[...] = t_all[...].reshape(CP, PIX).T
    for d in (3, 2):
        b.second[d][1].wait_recv()
    for d in (0, 1):
        b.second[d][3].wait_recv()
    squares = squares_of(x) + squares_of(at2(b, 1)) + squares_of(at2(b, 3))
    for d in (0, 3, 1, 2):
        a.far[d].wait_recv()
    first_half(at2(a, 2))
    for d in (0, 3, 1, 2):
        b.far[d].wait_recv()
    norm_row[0] = squares + squares_of(at2(b, 2))
    n_copy = send(norm_row.at[0], norm_in, peer(dc=1))

    raw_copies = []
    for low, high in CUTS:
        cols = slice(low, high)
        value = dot(
            hid[...].reshape(HT, PIX), wb[:, :, :, cols].reshape(HT, high - low), TN
        )
        raw[:, cols] = value
        raw_out[:, cols] = value.astype(BF16)
        part = pl.ds(low, high - low)
        raw_copies.append(send(raw_out.at[:, part], raw_in.at[:, part], peer(dc=1)))

    n_copy.wait_recv()
    norm = jnp.sum(norm_row[0] + norm_in[...], axis=0, keepdims=True)
    inv_row = lax.rsqrt(norm + 1.0)
    norm_row[1] = jnp.broadcast_to(inv_row, (8, CP))
    for copy, (low, high) in zip(raw_copies, CUTS):
        copy.wait_recv()
        cols = slice(low, high)
        sums = jnp.zeros((8, high - low), F32)
        inv = norm_row[1][0:1, cols]
        for q in range(8):
            rows = slice(q * 32, (q + 1) * 32)
            total = raw[rows, cols] + raw_in[rows, cols].astype(F32)
            state = s_tok[rows, cols].astype(F32)
            target = t_tok[rows, cols].astype(F32)
            grad = KEEP_COEF * state + ADD_COEF * (total * inv) - target
            dbranch = (ADD_COEF / SAMPLES * grad).astype(BF16)
            dbr[rows, cols] = dbranch
            wide = dbranch.astype(F32)
            dbn[rows, cols] = (wide * inv).astype(BF16)
            sums = sums + jnp.sum((wide * total).reshape(4, 8, high - low), axis=0)
        dot_rows[:, cols] = jnp.broadcast_to(
            jnp.sum(sums, axis=0, keepdims=True), (8, high - low)
        )
    dot_high = dot_rows[0:1].astype(BF16).astype(F32)
    dot_low = dot_rows[0:1] - dot_high
    row = lax.broadcasted_iota(jnp.int32, (HP, 1), 0)

    def second_grad(slab):
        value = dot(hid[pl.ds(slab * 4, 4)].reshape(4 * HP, PIX), dbr[...], NN)
        for j in range(4):
            block = value[j * HP : (j + 1) * HP]
            block = jnp.where(row == HALF, dot_high, block)
            block = jnp.where(row == HALF + 1, dot_low, block)
            gb[slab, j] = block.astype(BF16)

    def first_grad(slab):
        for j in range(4):
            value = pre[slab * 4 + j]
            sig = jax.nn.sigmoid(value)
            slope = sig * (1.0 + value * (1.0 - sig))
            grad = dh[j * 4 + slab]
            dpre[j] = (grad * gain[slab * 4 + j] * slope * SILU_GAIN).astype(BF16)
        value = dot(dpre[...].reshape(4 * HP, PIX), s_tok[...], NN)
        ga[slab] = value.reshape(4, HP, CP).astype(BF16)

    def hidden_grad(i, _):
        dh[pl.ds(i * 4, 4)] = dot(wb[i].reshape(4 * HP, CP), dbn[...], NT).reshape(4, HP, PIX)
        return 0

    def scatter_far(s, d):
        s.got_half[d] = send(
            s.g.at[at2(s, 2), at1(s, d)], s.half2.at[d], s.p2(1 if d < 2 else 3)
        )

    def scatter_near(s, d):
        way, e = (1, 3) if d < 2 else (0, 1)
        s.got_full[way, d] = send(
            s.g.at[at2(s, e), at1(s, d)], s.full2.at[way, d], s.p2(e)
        )

    def scatter_relay(s, d):
        s.got_half[d].wait_recv()
        way, e = (0, 1) if d < 2 else (1, 3)
        spot = (at2(s, e), at1(s, d))
        s.g[spot] = (s.g[spot].astype(F32) + s.half2[d].astype(F32)).astype(BF16)
        s.got_full[way, d] = send(s.g.at[spot[0], spot[1]], s.full2.at[way, d], s.p2(e))

    def scatter_sum(s, d):
        s.got_full[0, d].wait_recv()
        s.got_full[1, d].wait_recv()
        spot = (s.i2, at1(s, d))
        total = (
            s.g[spot].astype(F32) + s.full2[0, d].astype(F32) + s.full2[1, d].astype(F32)
        )
        if d == 0:
            s.own = total
        else:
            s.g[spot] = total.astype(BF16)

    def ring_far(s):
        spot = s.g.at[s.i2, at1(s, 2)]
        low, high = pl.ds(0, s.cut), pl.ds(s.cut, HP - s.cut)
        s.far_up = send(spot.at[low], s.half1.at[low], s.p1(1))
        s.far_down = send(spot.at[high], s.half1.at[high], s.p1(3))
        s.near = []

    def ring_near(s, d):
        low, high = pl.ds(0, s.cut), pl.ds(s.cut, HP - s.cut)
        part, way = (high, 0) if d == 1 else (low, 1)
        s.near.append(send(s.g.at[s.i2, at1(s, d), part], s.full1.at[way, part], s.p1(d)))

    def ring_relay(s, d):
        part, way, copy = (
            (slice(0, s.cut), 0, s.far_up) if d == 1 else (slice(s.cut, HP), 1, s.far_down)
        )
        copy.wait_recv()
        at = at1(s, d)
        s.g[s.i2, at, part] = (
            s.g[s.i2, at, part].astype(F32) + s.half1[part].astype(F32)
        ).astype(BF16)
        rows = pl.ds(part.start, part.stop - part.start)
        s.near.append(send(s.g.at[s.i2, at, rows], s.full1.at[way, rows], s.p1(d)))

    def ring_sum(s):
        for copy in s.near:
            copy.wait_recv()
        return s.own + s.full1[0].astype(F32) + s.full1[1].astype(F32)

    def start(s, grad):
        s.got_half, s.got_full = {}, {}
        grad(at2(s, 2))
        scatter_far(s, 1)
        scatter_far(s, 2)
        grad(at2(s, 1))
        scatter_near(s, 2)
        grad(at2(s, 3))
        scatter_near(s, 1)
        scatter_far(s, 0)
        scatter_far(s, 3)

    start(b, second_grad)
    lax.fori_loop(0, 4, hidden_grad, 0)
    start(a, first_grad)
    for d in (1, 2, 0, 3):
        scatter_relay(b, d)
    scatter_near(b, 3)
    scatter_near(b, 0)
    second_grad(x)
    first_grad(y)
    for d in (1, 2, 0, 3):
        scatter_relay(a, d)
    scatter_near(a, 3)
    scatter_near(a, 0)
    for s in (b, a):
        scatter_sum(s, 2)
        ring_far(s)
        scatter_sum(s, 1)
        ring_near(s, 1)
        ring_relay(s, 1)
    for s in (b, a):
        scatter_sum(s, 3)
        ring_near(s, 3)
        ring_relay(s, 3)
        scatter_sum(s, 0)

    def hand_out(out, zs, zr):
        for q in range(ROWS):
            cols = slice(q * CHAN_PAD, (q + 1) * CHAN_PAD)
            fill = jnp.zeros((HP, WP - CHAN_PAD), F32)
            zs[q] = jnp.concatenate([out[:, cols], fill], axis=1).astype(BF16)
        zr[r] = zs[r]
        return [
            send(zs.at[((z + dz) % 4) * 2 + (c + dc) % 2], zr.at[r], peer(dz=dz, dc=dc))
            for dz, dc in group
        ]

    grad2 = ring_sum(b)
    w2 = wb[x, y].astype(F32)
    inv2 = norm_row[1][0:1]
    dot2 = grad2[HALF : HALF + 1] + grad2[HALF + 1 : HALF + 2]
    z2_copies = hand_out(grad2 * inv2 - w2 * (dot2 * inv2 * inv2 * inv2), zs2, zr2)
    grad1 = ring_sum(a)
    w1 = wa[y, x].astype(F32)
    inv1 = lax.rsqrt(jnp.sum(w1 * w1, axis=1, keepdims=True) + 1.0)
    dot1 = jnp.sum(w1 * grad1, axis=1, keepdims=True)
    z1_copies = hand_out(grad1 * inv1 - w1 * (dot1 * inv1 * inv1 * inv1), zs1, zr1)

    for copy in z2_copies:
        copy.wait_recv()
    for core in range(2):
        value = sum(zr2[2 * q + core].astype(F32) for q in range(4))
        out2[0, core * HALF : (core + 1) * HALF, :] = value[:HALF, :CHAN]
    for copy in z1_copies:
        copy.wait_recv()
    for core in range(2):
        value = sum(zr1[2 * q + core].astype(F32) for q in range(4))
        value = jnp.concatenate([value, jnp.zeros((128 - HP, WP), F32)], axis=0).T
        out1[0, :, core * HALF : (core + 1) * HALF] = value[:CHAN, :HALF]
    for copy in started:
        copy.wait_send()


def local(clean, noise, bucket, mod_table, w_first, w_second):
    vmem = pl.BlockSpec(memory_space=pltpu.VMEM)
    smem = pl.BlockSpec(memory_space=pltpu.SMEM)
    hbm = pl.BlockSpec(memory_space=pl.ANY)
    block = (HP, CP)
    return pl.pallas_call(
        kernel,
        out_shape=(
            jax.ShapeDtypeStruct((1, CHAN, BLOCK), F32),
            jax.ShapeDtypeStruct((1, BLOCK, CHAN), F32),
        ),
        in_specs=[hbm, hbm, smem, hbm, hbm, hbm],
        out_specs=(vmem, vmem),
        scratch_shapes=[
            pltpu.VMEM(clean.shape, F32),
            pltpu.VMEM(noise.shape, F32),
            pltpu.VMEM((BUCKETS, WIDTH), F32),
            pltpu.VMEM((CHAN, BLOCK), F32),
            pltpu.VMEM((BLOCK, CHAN), F32),
            pltpu.VMEM((2, HP, WP), BF16),
            pltpu.VMEM((2, HP, WP), BF16),
            pltpu.VMEM((ROWS, HP, WP), BF16),
            pltpu.VMEM((ROWS, HP, WP), BF16),
            pltpu.VMEM((4, CHAN_PAD, PIX), BF16),
            pltpu.VMEM((4, CHAN_PAD, PIX), BF16),
            pltpu.VMEM((ROWS, CHAN_PAD, PIX), BF16),
            pltpu.VMEM((ROWS, CHAN_PAD, PIX), BF16),
            pltpu.VMEM((PIX, CP), BF16),
            pltpu.VMEM((PIX, CP), BF16),
            pltpu.VMEM((4, 4, *block), BF16),
            pltpu.VMEM((4, 4, *block), BF16),
            pltpu.VMEM((4, 4, *block), BF16),
            pltpu.VMEM((4, 4, *block), BF16),
            pltpu.VMEM((4, *block), BF16),
            pltpu.VMEM((2, 4, *block), BF16),
            pltpu.VMEM(block, BF16),
            pltpu.VMEM((2, *block), BF16),
            pltpu.VMEM((4, *block), BF16),
            pltpu.VMEM((2, 4, *block), BF16),
            pltpu.VMEM(block, BF16),
            pltpu.VMEM((2, *block), BF16),
            pltpu.VMEM((16, HP, PIX), F32),
            pltpu.VMEM((16, HP, PIX), F32),
            pltpu.VMEM((16, HP, PIX), BF16),
            pltpu.VMEM((4, HP, PIX), BF16),
            pltpu.VMEM((PIX, CP), F32),
            pltpu.VMEM((PIX, CP), BF16),
            pltpu.VMEM((PIX, CP), BF16),
            pltpu.VMEM((2, 8, CP), F32),
            pltpu.VMEM((8, CP), F32),
            pltpu.VMEM((PIX, CP), BF16),
            pltpu.VMEM((PIX, CP), BF16),
            pltpu.VMEM((8, CP), F32),
            pltpu.VMEM((16, HP, PIX), F32),
            pltpu.VMEM((ROWS, HP, WP), BF16),
            pltpu.VMEM((ROWS, HP, WP), BF16),
            pltpu.VMEM((ROWS, HP, WP), BF16),
            pltpu.VMEM((ROWS, HP, WP), BF16),
            pltpu.SemaphoreType.DMA((5,)),
            pltpu.SemaphoreType.DMA((MAX_COPIES,)),
            pltpu.SemaphoreType.DMA((MAX_COPIES,)),
        ],
        compiler_params=pltpu.CompilerParams(
            collective_id=0, has_side_effects=True, vmem_limit_bytes=60 * 1024 * 1024
        ),
    )(clean, noise, bucket, mod_table, w_first, w_second)


def solution(mesh):
    in_specs = (
        P("row", "col"),
        P("row", "col"),
        P(),
        P(),
        P(None, "row", "col"),
        P(None, "col", "row"),
    )
    out_specs = (P(None, "row", "col"), P(None, "col", "row"))
    return jax.shard_map(local, mesh=mesh, in_specs=in_specs, out_specs=out_specs, check_vma=False)
```

time: 99.4 us -> 90.9 us (0.914)
  Pallas kernels: 92.3 us -> 86.2 us
  other arithmetic: 1.21 us -> 0 us
  local copies, waits for them, and re-layouts: 4.96 us -> 3.81 us
    pallas_call x1, Pallas kernels: 92.3 us -> 86.2 us  [local(): pl.pallas_call(kernel, out_shape=(jax.ShapeDtypeStruct((1, CHAN, BLOCK),...]
    pallas_call x0 -> x1, local copies, waits for them, and re-layouts: none -> 1.65 us  [local(): pl.pallas_call(kernel, out_shape=(jax.ShapeDtypeStruct((1, CHAN, BLOCK),...]
    pad x2 -> x0, local copies, waits for them, and re-layouts: 1.33 us -> none  [the longest x1 0.68 us: local(): mod = jnp.pad(mod_table[0], ((0, 0), (0, CP - WIDTH)))]
    slice x1 -> x0, local copies, waits for them, and re-layouts: 1.05 us -> none  [local(): second = part[:, :, CHAN_PAD:CHAN_PAD + CHAN].reshape(BLOCK, CHAN)]
    unnamed x5 -> x4, local copies, waits for them, and re-layouts: 1.67 us -> 2.16 us
where the time goes in v2:
time: 90.9 us; the launch traced here: 90.6 us
  Pallas kernels  86.2 us (95%)
  local copies, waits for them, and re-layouts  3.81 us (4%)
    pallas_call x1, Pallas kernels, local(): pl.pallas_call(kernel, out_shape=(jax.ShapeDtypeStruct((1, CHAN, BLOCK),...  86.2 us
    unnamed x4, local copies, waits for them, and re-layouts  2.16 us

profile of v2, /device:TPU:1, one launch (start us, length us, event | category | flops | bytes accessed | tf_op | source)
XLA Modules:
  0.0 90.6 jit_solution(1859290089878074678)
XLA Ops:
  0.6 1.5 %copy.8.w2_hbm = f32[1,84,168]{2,1,0:T(8,128)} copy(f32[1,84,168]{2,0,1:T(1,128)} %param.11) | data formatting | bytes 112896 | tf_op args[5]
  2.1 86.2 %shard_map.77 = (f32[1,168,84]{2,1,0:T(8,128)}, f32[1,84,168]{2,1,0:T(8,128)}) custom-call(f32[168,1024]{1,0:T(8,128)} %clean_hbm.1, f32[168,1024]{1,0:T(8,128)} %noise_hbm.1, s32[64]{0:T(128)} %bucket.1, f32[1,32,1344]{2,1,0:T(8,128)} %mod_hbm.1, f32[1,168,84]{2,1,0:T(8,128)} %w1_hbm.1, f32[1,84,168]{2,1,0:T(8,128)} %copy.8.w2_hbm), custom_call_target="tpu_custom_call" | custom-call | tf_op jit(solution)/shard_map/pallas_call | solution.py:494
  88.4 0.0 copy-start
  88.4 1.6 %copy.9 = f32[1,84,168]{2,0,1:T(1,128)} copy(f32[1,84,168]{2,1,0:T(8,128)} %get-tuple-element.3) | data formatting | bytes 112896 | tf_op jit(solution)/shard_map/pallas_call | solution.py:494
  90.0 0.0 copy-done
  90.0 0.6 copy.11
Async XLA Ops:
  88.4 1.7 %copy-start = (f32[1,168,84]{2,1,0:T(8,128)S(1)}, f32[1,168,84]{2,1,0:T(8,128)}, u32[]{:S(2)}) copy-start(f32[1,168,84]{2,1,0:T(8,128)} %get-tuple-element.6) | copy-start | bytes 169348

commit v3 on v2

--- a/solution.py
+++ b/solution.py
@@ -34,6 +34,59 @@
 NT = (((1,), (1,)), ((), ()))
 TN = (((0,), (0,)), ((), ()))
 MAX_COPIES = 160
+PLAN = (
+    ("grad", "b", 2),
+    ("hidden",),
+    ("far", "b", 1),
+    ("far", "b", 3),
+    ("grad", "a", 2),
+    ("far", "b", 2),
+    ("far", "b", 0),
+    ("far", "a", 1),
+    ("far", "a", 2),
+    ("far", "a", 3),
+    ("grad", "b", 3),
+    ("grad", "a", 3),
+    ("grad", "b", 1),
+    ("grad", "a", 1),
+    ("near", "a", 3),
+    ("near", "b", 3),
+    ("relay", "b", 3),
+    ("relay", "a", 2),
+    ("near", "b", 2),
+    ("grad", "a", 0),
+    ("near", "a", 2),
+    ("relay", "b", 2),
+    ("relay", "a", 3),
+    ("grad", "b", 0),
+    ("near", "a", 1),
+    ("near", "b", 1),
+    ("far", "a", 0),
+    ("relay", "b", 1),
+    ("relay", "a", 1),
+    ("sum", "b", 2),
+    ("sum", "a", 2),
+    ("ring_far", "a"),
+    ("ring_far", "b"),
+    ("near", "b", 0),
+    ("near", "a", 0),
+    ("relay", "b", 0),
+    ("relay", "a", 0),
+    ("sum", "b", 1),
+    ("ring_near", "b", 1),
+    ("sum", "b", 3),
+    ("sum", "a", 1),
+    ("ring_relay", "b", 1),
+    ("sum", "a", 3),
+    ("ring_near", "a", 1),
+    ("ring_near", "a", 3),
+    ("ring_near", "b", 3),
+    ("ring_relay", "a", 3),
+    ("ring_relay", "b", 3),
+    ("ring_relay", "a", 1),
+    ("sum", "a", 0),
+    ("sum", "b", 0),
+)
 
 
 def dot(a, b, dims):
@@ -87,7 +140,7 @@
         for i, (src, dst) in enumerate(
             (
                 (w1_hbm.at[0], w1_in),
-                (w2_hbm.at[0], w2_in),
+                (w2_hbm.at[:, 0], w2_in),
                 (clean_hbm, clean),
                 (noise_hbm, noise),
                 (mod_hbm.at[0], mod),
@@ -128,6 +181,14 @@
             jnp.concatenate([target, pad], axis=0).astype(BF16),
         )
 
+    pl.semaphore_wait(barrier, len(near))
+
+    w1_copies = [
+        send(w1_out.at[(c + dc) % 2], w1_got.at[r], peer(dz=dz, dc=dc)) for dz, dc in group
+    ]
+    w2_copies = [
+        send(w2_out.at[(c + dc) % 2], w2_got.at[r], peer(dz=dz, dc=dc)) for dz, dc in group
+    ]
     loads[2].wait()
     loads[3].wait()
     loads[4].wait()
@@ -137,15 +198,6 @@
         tg[d] = target
     s_all[r] = st[0]
     t_all[r] = tg[0]
-
-    pl.semaphore_wait(barrier, len(near))
-
-    w1_copies = [
-        send(w1_out.at[(c + dc) % 2], w1_got.at[r], peer(dz=dz, dc=dc)) for dz, dc in group
-    ]
-    w2_copies = [
-        send(w2_out.at[(c + dc) % 2], w2_got.at[r], peer(dz=dz, dc=dc)) for dz, dc in group
-    ]
     s_copies = {d: send(st.at[d], s_all.at[r], peer(dz=d)) for d in (2, 1, 3)}
     s_own = send(st.at[0], s_all.at[r], peer(dc=1))
     t_copies = {d: send(tg.at[d], t_all.at[r], peer(dz=d)) for d in (2, 1, 3)}
@@ -388,7 +440,6 @@
         low, high = pl.ds(0, s.cut), pl.ds(s.cut, HP - s.cut)
         s.far_up = send(spot.at[low], s.half1.at[low], s.p1(1))
         s.far_down = send(spot.at[high], s.half1.at[high], s.p1(3))
-        s.near = []
 
     def ring_near(s, d):
         low, high = pl.ds(0, s.cut), pl.ds(s.cut, HP - s.cut)
@@ -412,42 +463,26 @@
             copy.wait_recv()
         return s.own + s.full1[0].astype(F32) + s.full1[1].astype(F32)
 
-    def start(s, grad):
-        s.got_half, s.got_full = {}, {}
-        grad(at2(s, 2))
-        scatter_far(s, 1)
-        scatter_far(s, 2)
-        grad(at2(s, 1))
-        scatter_near(s, 2)
-        grad(at2(s, 3))
-        scatter_near(s, 1)
-        scatter_far(s, 0)
-        scatter_far(s, 3)
-
-    start(b, second_grad)
-    lax.fori_loop(0, 4, hidden_grad, 0)
-    start(a, first_grad)
-    for d in (1, 2, 0, 3):
-        scatter_relay(b, d)
-    scatter_near(b, 3)
-    scatter_near(b, 0)
-    second_grad(x)
-    first_grad(y)
-    for d in (1, 2, 0, 3):
-        scatter_relay(a, d)
-    scatter_near(a, 3)
-    scatter_near(a, 0)
-    for s in (b, a):
-        scatter_sum(s, 2)
-        ring_far(s)
-        scatter_sum(s, 1)
-        ring_near(s, 1)
-        ring_relay(s, 1)
-    for s in (b, a):
-        scatter_sum(s, 3)
-        ring_near(s, 3)
-        ring_relay(s, 3)
-        scatter_sum(s, 0)
+    sides = {"a": a, "b": b}
+    for s in (a, b):
+        s.got_half, s.got_full, s.near = {}, {}, []
+    steps = {
+        "far": scatter_far,
+        "near": scatter_near,
+        "relay": scatter_relay,
+        "sum": scatter_sum,
+        "ring_far": ring_far,
+        "ring_near": ring_near,
+        "ring_relay": ring_relay,
+    }
+    for step, *at in PLAN:
+        if step == "hidden":
+            lax.fori_loop(0, 4, hidden_grad, 0)
+        elif step == "grad":
+            side = sides[at[0]]
+            (first_grad if side is a else second_grad)(at2(side, at[1]))
+        else:
+            steps[step](sides[at[0]], *at[1:])
 
     def hand_out(out, zs, zr):
         for q in range(ROWS):
@@ -475,7 +510,7 @@
         copy.wait_recv()
     for core in range(2):
         value = sum(zr2[2 * q + core].astype(F32) for q in range(4))
-        out2[0, core * HALF : (core + 1) * HALF, :] = value[:HALF, :CHAN]
+        out2[core * HALF : (core + 1) * HALF, 0, :] = value[:HALF, :CHAN]
     for copy in z1_copies:
         copy.wait_recv()
     for core in range(2):
@@ -491,11 +526,11 @@
     smem = pl.BlockSpec(memory_space=pltpu.SMEM)
     hbm = pl.BlockSpec(memory_space=pl.ANY)
     block = (HP, CP)
-    return pl.pallas_call(
+    first, second = pl.pallas_call(
         kernel,
         out_shape=(
             jax.ShapeDtypeStruct((1, CHAN, BLOCK), F32),
-            jax.ShapeDtypeStruct((1, BLOCK, CHAN), F32),
+            jax.ShapeDtypeStruct((BLOCK, 1, CHAN), F32),
         ),
         in_specs=[hbm, hbm, smem, hbm, hbm, hbm],
         out_specs=(vmem, vmem),
@@ -551,7 +586,8 @@
         compiler_params=pltpu.CompilerParams(
             collective_id=0, has_side_effects=True, vmem_limit_bytes=60 * 1024 * 1024
         ),
-    )(clean, noise, bucket, mod_table, w_first, w_second)
+    )(clean, noise, bucket, mod_table, w_first, jnp.transpose(w_second, (1, 0, 2)))
+    return first, jnp.transpose(second, (1, 0, 2))
 
 
 def solution(mesh):

time: 90.9 us -> 83.1 us (0.914)
  Pallas kernels: 86.2 us -> 80.1 us
  local copies, waits for them, and re-layouts: 3.81 us -> 2.2 us
    pallas_call x1, Pallas kernels: 86.2 us -> 80.1 us  [local(): pl.pallas_call(kernel, out_shape=(jax.ShapeDtypeStruct((1, CHAN, BLOCK),...]
    pallas_call x1 -> x0, local copies, waits for them, and re-layouts: 1.65 us -> none  [local(): pl.pallas_call(kernel, out_shape=(jax.ShapeDtypeStruct((1, CHAN, BLOCK),...]
where the time goes in v3:
time: 83.1 us; the launch traced here: 82.9 us
  Pallas kernels  80.1 us (96%)
  local copies, waits for them, and re-layouts  2.2 us (3%)
    pallas_call x1, Pallas kernels, local(): pl.pallas_call(kernel, out_shape=(jax.ShapeDtypeStruct((1, CHAN, BLOCK),...  80.1 us
    unnamed x4, local copies, waits for them, and re-layouts  2.2 us

profile of v3, /device:TPU:1, one launch (start us, length us, event | category | flops | bytes accessed | tf_op | source)
XLA Modules:
  0.0 82.9 jit_solution(13921985476398120258)
XLA Ops:
  0.6 80.1 %shard_map.77 = (f32[1,168,84]{2,1,0:T(8,128)}, f32[84,1,168]{2,1,0:T(1,128)}) custom-call(f32[168,1024]{1,0:T(8,128)} %clean_hbm.1, f32[168,1024]{1,0:T(8,128)} %noise_hbm.1, s32[64]{0:T(128)} %bucket.1, f32[1,32,1344]{2,1,0:T(8,128)} %mod_hbm.1, f32[1,168,84]{2,1,0:T(8,128)} %w1_hbm.1, f32[84,1,168]{2,1,0:T(1,128)} %bitcast.3), custom_call_target="tpu_custom_call" | custom-call | tf_op jit(solution)/shard_map/pallas_call | solution.py:529
  80.7 0.0 copy-start
  80.7 1.6 %copy.10 = f32[1,168,84]{2,1,0:T(8,128)} copy(f32[1,168,84]{2,1,0:T(8,128)} %get-tuple-element.8) | data formatting | bytes 112896
  82.3 0.0 copy-done
  82.3 0.6 copy.11
Async XLA Ops:
  80.7 1.6 %copy-start = (f32[84,1,168]{2,1,0:T(1,128)S(1)}, f32[84,1,168]{2,1,0:T(1,128)}, u32[]{:S(2)}) copy-start(f32[84,1,168]{2,1,0:T(1,128)} %get-tuple-element.5) | copy-start | bytes 169348

commit v4 on v3

--- a/solution.py
+++ b/solution.py
@@ -28,7 +28,7 @@
 HALF = BLOCK // 2
 HP = 48
 HT = 16 * HP
-WP = 256
+FOLD = HP + HP // 3
 CUTS = ((0, 768), (768, 1408))
 NN = (((1,), (0,)), ((), ()))
 NT = (((1,), (1,)), ((), ()))
@@ -36,67 +36,82 @@
 MAX_COPIES = 160
 PLAN = (
     ("grad", "b", 2),
+    ("far", "b", 0),
+    ("far", "b", 2),
     ("hidden",),
-    ("far", "b", 1),
-    ("far", "b", 3),
     ("grad", "a", 2),
-    ("far", "b", 2),
-    ("far", "b", 0),
     ("far", "a", 1),
     ("far", "a", 2),
+    ("grad", "a", 1),
+    ("far", "b", 3),
+    ("far", "b", 1),
     ("far", "a", 3),
-    ("grad", "b", 3),
-    ("grad", "a", 3),
+    ("near", "a", 2),
     ("grad", "b", 1),
-    ("grad", "a", 1),
-    ("near", "a", 3),
-    ("near", "b", 3),
-    ("relay", "b", 3),
-    ("relay", "a", 2),
     ("near", "b", 2),
     ("grad", "a", 0),
-    ("near", "a", 2),
+    ("grad", "b", 3),
     ("relay", "b", 2),
-    ("relay", "a", 3),
+    ("near", "a", 3),
+    ("grad", "a", 3),
     ("grad", "b", 0),
     ("near", "a", 1),
     ("near", "b", 1),
+    ("relay", "b", 3),
+    ("relay", "b", 1),
+    ("relay", "a", 2),
+    ("relay", "a", 1),
+    ("near", "b", 3),
+    ("relay", "b", 0),
+    ("near", "b", 0),
+    ("sum", "b", 2),
+    ("ring_far", "b"),
+    ("relay", "a", 3),
+    ("sum", "b", 1),
     ("far", "a", 0),
-    ("relay", "b", 1),
-    ("relay", "a", 1),
-    ("sum", "b", 2),
     ("sum", "a", 2),
     ("ring_far", "a"),
-    ("ring_far", "b"),
-    ("near", "b", 0),
+    ("sum", "b", 3),
+    ("ring_near", "b", 1),
+    ("ring_near", "b", 3),
+    ("ring_relay", "b", 1),
+    ("ring_relay", "b", 3),
+    ("sum", "a", 1),
+    ("relay", "a", 0),
+    ("sum", "b", 0),
     ("near", "a", 0),
-    ("relay", "b", 0),
-    ("relay", "a", 0),
-    ("sum", "b", 1),
-    ("ring_near", "b", 1),
-    ("sum", "b", 3),
-    ("sum", "a", 1),
-    ("ring_relay", "b", 1),
     ("sum", "a", 3),
+    ("ring_relay", "a", 3),
     ("ring_near", "a", 1),
+    ("ring_relay", "a", 1),
     ("ring_near", "a", 3),
-    ("ring_near", "b", 3),
-    ("ring_relay", "a", 3),
-    ("ring_relay", "b", 3),
-    ("ring_relay", "a", 1),
+    ("finish", "b"),
     ("sum", "a", 0),
-    ("sum", "b", 0),
+    ("finish", "a"),
 )
 
 
 def dot(a, b, dims):
     return lax.dot_general(a, b, dims, preferred_element_type=F32)
+
+
+def fold(block):
+    third, rest = HP // 3, CHAN - 128
+    below = [block[i * third : (i + 1) * third, 128:CHAN] for i in range(3)]
+    below.append(jnp.zeros((third, 128 - 3 * rest), F32))
+    return jnp.concatenate([block[:, :128], jnp.concatenate(below, axis=1)], axis=0)
+
+
+def unfold(block):
+    rest = CHAN - 128
+    right = [block[HP:, i * rest : (i + 1) * rest] for i in range(3)]
+    return jnp.concatenate([block[:HP], jnp.concatenate(right, axis=0)], axis=1)
 
 
 def kernel(
     clean_hbm, noise_hbm, bucket, mod_hbm, w1_hbm, w2_hbm, out1, out2,
     clean, noise, mod, w1_in, w2_in, w1_out, w2_out, w1_got, w2_got,
-    st, tg, s_all, t_all, s_tok, t_tok, wa, wb, ga, gb,
+    st, tg, s_all, t_all, s_tok, base, wa, wb, ga, gb,
     ra1, ra2, rx1, rx2, rb1, rb2, ry1, ry2,
     gain, pre, hid, dpre, raw, raw_out, raw_in, norm_row, norm_in,
     dbr, dbn, dot_rows, dh, zs1, zs2, zr1, zr2, load_sems, send_sems, recv_sems,
@@ -159,9 +174,8 @@
     for core in range(2):
         pick = (col_of == hid_of + HALF * core) & (hid_of < HALF)
         pick = jnp.where(pick, 1.0, 0.0).astype(BF16)
-        fill = jnp.zeros((HP, WP - CHAN), F32)
-        w1_out[core] = jnp.concatenate([dot(pick, w1_bf, NT), fill], axis=1).astype(BF16)
-        w2_out[core] = jnp.concatenate([dot(pick, w2_bf, NN), fill], axis=1).astype(BF16)
+        w1_out[core] = fold(dot(pick, w1_bf, NT)).astype(BF16)
+        w2_out[core] = fold(dot(pick, w2_bf, NN)).astype(BF16)
     w1_got[r] = w1_out[c]
     w2_got[r] = w2_out[c]
 
@@ -252,9 +266,11 @@
     for s, copies, got in ((a, w1_copies, w1_got), (b, w2_copies, w2_got)):
         for copy in copies:
             copy.wait_recv()
-        s.w[s.i2, s.i1] = jnp.concatenate(
-            [got[q][:, :CHAN_PAD].astype(F32) for q in range(ROWS)], axis=1
-        ).astype(BF16)
+        fill = jnp.zeros((HP, CHAN_PAD - CHAN), F32)
+        parts = []
+        for q in range(ROWS):
+            parts += [unfold(got[q].astype(F32)), fill]
+        s.w[s.i2, s.i1] = jnp.concatenate(parts, axis=1).astype(BF16)
         block = s.w.at[s.i2, s.i1]
         s.first = {d: send(block, block, s.p1(d)) for d in (1, 3)}
         s.second = {}
@@ -331,7 +347,7 @@
     t_own.wait_recv()
     for d in (2, 1, 3):
         t_copies[d + 4].wait_recv()
-    t_tok[...] = t_all[...].reshape(CP, PIX).T
+    base[...] = KEEP_COEF * s_tok[...].astype(F32) - t_all[...].reshape(CP, PIX).T.astype(F32)
     for d in (3, 2):
         b.second[d][1].wait_recv()
     for d in (0, 1):
@@ -340,21 +356,25 @@
     for d in (0, 3, 1, 2):
         a.far[d].wait_recv()
     first_half(at2(a, 2))
+    def branch(slab, cols):
+        weights = wb[slab, :, :, cols].reshape(4 * HP, cols.stop - cols.start)
+        return dot(hid[pl.ds(slab * 4, 4)].reshape(4 * HP, PIX), weights, TN)
+
+    for cut in CUTS:
+        cols = slice(*cut)
+        raw[:, cols] = branch(x, cols) + branch(at2(b, 1), cols) + branch(at2(b, 3), cols)
     for d in (0, 3, 1, 2):
         b.far[d].wait_recv()
+    raw_copies = []
+    for cut in CUTS:
+        cols = slice(*cut)
+        value = raw[:, cols] + branch(at2(b, 2), cols)
+        raw[:, cols] = value
+        raw_out[:, cols] = value.astype(BF16)
+        part = pl.ds(cut[0], cut[1] - cut[0])
+        raw_copies.append(send(raw_out.at[:, part], raw_in.at[:, part], peer(dc=1)))
     norm_row[0] = squares + squares_of(at2(b, 2))
     n_copy = send(norm_row.at[0], norm_in, peer(dc=1))
-
-    raw_copies = []
-    for low, high in CUTS:
-        cols = slice(low, high)
-        value = dot(
-            hid[...].reshape(HT, PIX), wb[:, :, :, cols].reshape(HT, high - low), TN
-        )
-        raw[:, cols] = value
-        raw_out[:, cols] = value.astype(BF16)
-        part = pl.ds(low, high - low)
-        raw_copies.append(send(raw_out.at[:, part], raw_in.at[:, part], peer(dc=1)))
 
     n_copy.wait_recv()
     norm = jnp.sum(norm_row[0] + norm_in[...], axis=0, keepdims=True)
@@ -364,18 +384,15 @@
         copy.wait_recv()
         cols = slice(low, high)
         sums = jnp.zeros((8, high - low), F32)
-        inv = norm_row[1][0:1, cols]
+        inv = norm_row[1][0:1, cols] * ADD_COEF
         for q in range(8):
             rows = slice(q * 32, (q + 1) * 32)
             total = raw[rows, cols] + raw_in[rows, cols].astype(F32)
-            state = s_tok[rows, cols].astype(F32)
-            target = t_tok[rows, cols].astype(F32)
-            grad = KEEP_COEF * state + ADD_COEF * (total * inv) - target
-            dbranch = (ADD_COEF / SAMPLES * grad).astype(BF16)
+            grad = base[rows, cols] + total * inv
+            dbranch = (ADD_COEF * grad).astype(BF16)
             dbr[rows, cols] = dbranch
-            wide = dbranch.astype(F32)
-            dbn[rows, cols] = (wide * inv).astype(BF16)
-            sums = sums + jnp.sum((wide * total).reshape(4, 8, high - low), axis=0)
+            product = dbranch.astype(F32) * total
+            sums = sums + jnp.sum(product.reshape(4, 8, high - low), axis=0)
         dot_rows[:, cols] = jnp.broadcast_to(
             jnp.sum(sums, axis=0, keepdims=True), (8, high - low)
         )
@@ -475,47 +492,55 @@
         "ring_near": ring_near,
         "ring_relay": ring_relay,
     }
+    def hand_out(out, zs, zr):
+        for q in range(ROWS):
+            first = q * CHAN_PAD
+            zs[q] = fold(out[:, first : first + CHAN]).astype(BF16)
+        zr[r] = zs[r]
+        return [
+            send(zs.at[((z + dz) % 4) * 2 + (c + dc) % 2], zr.at[r], peer(dz=dz, dc=dc))
+            for dz, dc in group
+        ]
+
+    def finish_second():
+        grad2 = ring_sum(b)
+        w2 = wb[x, y].astype(F32)
+        inv2 = norm_row[1][0:1]
+        dot2 = grad2[HALF : HALF + 1] + grad2[HALF + 1 : HALF + 2]
+        return hand_out(grad2 * inv2 - w2 * (dot2 * inv2 * inv2 * inv2), zs2, zr2)
+
+    def finish_first():
+        grad1 = ring_sum(a)
+        w1 = wa[y, x].astype(F32)
+        inv1 = lax.rsqrt(jnp.sum(w1 * w1, axis=1, keepdims=True) + 1.0)
+        dot1 = jnp.sum(w1 * grad1, axis=1, keepdims=True)
+        return hand_out(grad1 * inv1 - w1 * (dot1 * inv1 * inv1 * inv1), zs1, zr1)
+
     for step, *at in PLAN:
         if step == "hidden":
+            dbn[...] = (dbr[...].astype(F32) * norm_row[1][0:1]).astype(BF16)
             lax.fori_loop(0, 4, hidden_grad, 0)
+        elif step == "finish" and at[0] == "b":
+            z2_copies = finish_second()
+        elif step == "finish":
+            z1_copies = finish_first()
         elif step == "grad":
             side = sides[at[0]]
             (first_grad if side is a else second_grad)(at2(side, at[1]))
         else:
             steps[step](sides[at[0]], *at[1:])
 
-    def hand_out(out, zs, zr):
-        for q in range(ROWS):
-            cols = slice(q * CHAN_PAD, (q + 1) * CHAN_PAD)
-            fill = jnp.zeros((HP, WP - CHAN_PAD), F32)
-            zs[q] = jnp.concatenate([out[:, cols], fill], axis=1).astype(BF16)
-        zr[r] = zs[r]
-        return [
-            send(zs.at[((z + dz) % 4) * 2 + (c + dc) % 2], zr.at[r], peer(dz=dz, dc=dc))
-            for dz, dc in group
-        ]
-
-    grad2 = ring_sum(b)
-    w2 = wb[x, y].astype(F32)
-    inv2 = norm_row[1][0:1]
-    dot2 = grad2[HALF : HALF + 1] + grad2[HALF + 1 : HALF + 2]
-    z2_copies = hand_out(grad2 * inv2 - w2 * (dot2 * inv2 * inv2 * inv2), zs2, zr2)
-    grad1 = ring_sum(a)
-    w1 = wa[y, x].astype(F32)
-    inv1 = lax.rsqrt(jnp.sum(w1 * w1, axis=1, keepdims=True) + 1.0)
-    dot1 = jnp.sum(w1 * grad1, axis=1, keepdims=True)
-    z1_copies = hand_out(grad1 * inv1 - w1 * (dot1 * inv1 * inv1 * inv1), zs1, zr1)
-
     for copy in z2_copies:
         copy.wait_recv()
     for core in range(2):
-        value = sum(zr2[2 * q + core].astype(F32) for q in range(4))
-        out2[core * HALF : (core + 1) * HALF, 0, :] = value[:HALF, :CHAN]
+        value = unfold(sum(zr2[2 * q + core].astype(F32) for q in range(4)))
+        out2[core * HALF : (core + 1) * HALF, 0, :] = value[:HALF]
     for copy in z1_copies:
         copy.wait_recv()
     for core in range(2):
-        value = sum(zr1[2 * q + core].astype(F32) for q in range(4))
-        value = jnp.concatenate([value, jnp.zeros((128 - HP, WP), F32)], axis=0).T
+        value = unfold(sum(zr1[2 * q + core].astype(F32) for q in range(4)))
+        value = jnp.concatenate([value, jnp.zeros((HP, 256 - CHAN), F32)], axis=1)
+        value = jnp.concatenate([value, jnp.zeros((128 - HP, 256), F32)], axis=0).T
         out1[0, :, core * HALF : (core + 1) * HALF] = value[:CHAN, :HALF]
     for copy in started:
         copy.wait_send()
@@ -540,16 +565,16 @@
             pltpu.VMEM((BUCKETS, WIDTH), F32),
             pltpu.VMEM((CHAN, BLOCK), F32),
             pltpu.VMEM((BLOCK, CHAN), F32),
-            pltpu.VMEM((2, HP, WP), BF16),
-            pltpu.VMEM((2, HP, WP), BF16),
-            pltpu.VMEM((ROWS, HP, WP), BF16),
-            pltpu.VMEM((ROWS, HP, WP), BF16),
+            pltpu.VMEM((2, FOLD, 128), BF16),
+            pltpu.VMEM((2, FOLD, 128), BF16),
+            pltpu.VMEM((ROWS, FOLD, 128), BF16),
+            pltpu.VMEM((ROWS, FOLD, 128), BF16),
             pltpu.VMEM((4, CHAN_PAD, PIX), BF16),
             pltpu.VMEM((4, CHAN_PAD, PIX), BF16),
             pltpu.VMEM((ROWS, CHAN_PAD, PIX), BF16),
             pltpu.VMEM((ROWS, CHAN_PAD, PIX), BF16),
             pltpu.VMEM((PIX, CP), BF16),
-            pltpu.VMEM((PIX, CP), BF16),
+            pltpu.VMEM((PIX, CP), F32),
             pltpu.VMEM((4, 4, *block), BF16),
             pltpu.VMEM((4, 4, *block), BF16),
             pltpu.VMEM((4, 4, *block), BF16),
@@ -575,10 +600,10 @@
             pltpu.VMEM((PIX, CP), BF16),
             pltpu.VMEM((8, CP), F32),
             pltpu.VMEM((16, HP, PIX), F32),
-            pltpu.VMEM((ROWS, HP, WP), BF16),
-            pltpu.VMEM((ROWS, HP, WP), BF16),
-            pltpu.VMEM((ROWS, HP, WP), BF16),
-            pltpu.VMEM((ROWS, HP, WP), BF16),
+            pltpu.VMEM((ROWS, FOLD, 128), BF16),
+            pltpu.VMEM((ROWS, FOLD, 128), BF16),
+            pltpu.VMEM((ROWS, FOLD, 128), BF16),
+            pltpu.VMEM((ROWS, FOLD, 128), BF16),
             pltpu.SemaphoreType.DMA((5,)),
             pltpu.SemaphoreType.DMA((MAX_COPIES,)),
             pltpu.SemaphoreType.DMA((MAX_COPIES,)),
@@ -587,7 +612,7 @@
             collective_id=0, has_side_effects=True, vmem_limit_bytes=60 * 1024 * 1024
         ),
     )(clean, noise, bucket, mod_table, w_first, jnp.transpose(w_second, (1, 0, 2)))
-    return first, jnp.transpose(second, (1, 0, 2))
+    return first / SAMPLES, jnp.transpose(second / SAMPLES, (1, 0, 2))
 
 
 def solution(mesh):

time: 83.1 us -> 80 us (0.963)
  Pallas kernels: 80.1 us -> 76.9 us
  other arithmetic: 0 us -> 2.27 us
  local copies, waits for them, and re-layouts: 2.2 us -> 0.01 us
    pallas_call x1, Pallas kernels: 80.1 us -> 76.9 us  [local(): pl.pallas_call(kernel, out_shape=(jax.ShapeDtypeStruct((1, CHAN, BLOCK),...]
    unnamed x4 -> x2, local copies, waits for them, and re-layouts: 2.2 us -> 0.01 us
    div x0 -> x1, other arithmetic: none -> 1.56 us  [local(): return (first / SAMPLES, jnp.transpose(second / SAMPLES, (1, 0, 2)))]
where the time goes in v4:
time: 80 us; the launch traced here: 79.9 us
  Pallas kernels  76.9 us (96%)
  other arithmetic  2.27 us (3%)
    pallas_call x1, Pallas kernels, local(): pl.pallas_call(kernel, out_shape=(jax.ShapeDtypeStruct((1, CHAN, BLOCK),...  76.9 us

profile of v4, /device:TPU:1, one launch (start us, length us, event | category | flops | bytes accessed | tf_op | source)
XLA Modules:
  0.0 79.9 jit_solution(9867655042575523319)
XLA Ops:
  0.6 76.9 %shard_map.77 = (f32[1,168,84]{2,1,0:T(8,128)}, f32[84,1,168]{2,1,0:T(1,128)}) custom-call(f32[168,1024]{1,0:T(8,128)} %clean_hbm.1, f32[168,1024]{1,0:T(8,128)} %noise_hbm.1, s32[64]{0:T(128)} %bucket.1, f32[1,32,1344]{2,1,0:T(8,128)} %mod_hbm.1, f32[1,168,84]{2,1,0:T(8,128)} %w1_hbm.1, f32[84,1,168]{2,1,0:T(1,128)} %bitcast.3), custom_call_target="tpu_custom_call" | custom-call | tf_op jit(solution)/shard_map/pallas_call | solution.py:554
  77.6 0.0 copy-start
  77.6 1.6 %broadcast_multiply_fusion = f32[1,168,84]{2,1,0:T(8,128)} fusion(f32[1,168,84]{2,1,0:T(8,128)} %get-tuple-element.4), kind=kLoop, calls=%fused_computation.1 | loop fusion | flops 14112 | bytes 112896 | tf_op jit(solution)/shard_map/div | solution.py:615
  79.1 0.0 copy-done
  79.1 0.7 multiply_bitcast_fusion
Async XLA Ops:
  77.6 1.6 %copy-start = (f32[84,1,168]{2,1,0:T(1,128)S(1)}, f32[84,1,168]{2,1,0:T(1,128)}, u32[]{:S(2)}) copy-start(f32[84,1,168]{2,1,0:T(1,128)} %get-tuple-element.5) | copy-start | bytes 169348

commit v5 on v4

--- a/solution.py
+++ b/solution.py
@@ -28,6 +28,10 @@
 HALF = BLOCK // 2
 HP = 48
 HT = 16 * HP
+STRIPS = CP // 128
+FULL = 40
+SIZE_W = STRIPS * FULL + 24
+SIZE_G = STRIPS * FULL + 40
 FOLD = HP + HP // 3
 CUTS = ((0, 768), (768, 1408))
 NN = (((1,), (0,)), ((), ()))
@@ -36,55 +40,55 @@
 MAX_COPIES = 160
 PLAN = (
     ("grad", "b", 2),
+    ("far", "b", 2),
+    ("far", "b", 3),
+    ("far", "b", 1),
     ("far", "b", 0),
-    ("far", "b", 2),
     ("hidden",),
     ("grad", "a", 2),
     ("far", "a", 1),
     ("far", "a", 2),
-    ("grad", "a", 1),
-    ("far", "b", 3),
-    ("far", "b", 1),
-    ("far", "a", 3),
-    ("near", "a", 2),
-    ("grad", "b", 1),
-    ("near", "b", 2),
-    ("grad", "a", 0),
-    ("grad", "b", 3),
-    ("relay", "b", 2),
-    ("near", "a", 3),
     ("grad", "a", 3),
     ("grad", "b", 0),
+    ("grad", "a", 1),
+    ("far", "a", 0),
+    ("grad", "b", 3),
+    ("grad", "b", 1),
+    ("far", "a", 3),
+    ("grad", "a", 0),
+    ("relay", "b", 2),
+    ("near", "b", 2),
     ("near", "a", 1),
-    ("near", "b", 1),
+    ("near", "a", 2),
+    ("near", "b", 3),
+    ("relay", "b", 1),
     ("relay", "b", 3),
-    ("relay", "b", 1),
+    ("relay", "a", 1),
     ("relay", "a", 2),
-    ("relay", "a", 1),
-    ("near", "b", 3),
-    ("relay", "b", 0),
-    ("near", "b", 0),
     ("sum", "b", 2),
     ("ring_far", "b"),
+    ("near", "a", 3),
+    ("near", "b", 1),
+    ("near", "b", 0),
+    ("relay", "b", 0),
     ("relay", "a", 3),
+    ("sum", "a", 2),
+    ("sum", "b", 3),
+    ("ring_far", "a"),
     ("sum", "b", 1),
-    ("far", "a", 0),
-    ("sum", "a", 2),
-    ("ring_far", "a"),
-    ("sum", "b", 3),
     ("ring_near", "b", 1),
     ("ring_near", "b", 3),
     ("ring_relay", "b", 1),
+    ("relay", "a", 0),
     ("ring_relay", "b", 3),
+    ("near", "a", 0),
     ("sum", "a", 1),
-    ("relay", "a", 0),
-    ("sum", "b", 0),
-    ("near", "a", 0),
     ("sum", "a", 3),
-    ("ring_relay", "a", 3),
+    ("ring_near", "a", 3),
     ("ring_near", "a", 1),
     ("ring_relay", "a", 1),
-    ("ring_near", "a", 3),
+    ("sum", "b", 0),
+    ("ring_relay", "a", 3),
     ("finish", "b"),
     ("sum", "a", 0),
     ("finish", "a"),
@@ -108,10 +112,34 @@
     return jnp.concatenate([block[:HP], jnp.concatenate(right, axis=0)], axis=1)
 
 
+def pack(block, ref, at):
+    size = ref.shape[2]
+    left = (size - STRIPS * FULL) // STRIPS
+    rest = []
+    for j in range(STRIPS):
+        lanes = slice(128 * j, 128 * (j + 1))
+        ref[(*at, slice(FULL * j, FULL * (j + 1)))] = block[:FULL, lanes].astype(BF16)
+        rest.append(block[FULL : FULL + left, lanes])
+    fill = size - STRIPS * (FULL + left)
+    rest.append(jnp.zeros((fill, 128), F32))
+    ref[(*at, slice(STRIPS * FULL, size))] = jnp.concatenate(rest, axis=0).astype(BF16)
+
+
+def unpack(strips):
+    left = (strips.shape[0] - STRIPS * FULL) // STRIPS
+    fill = jnp.zeros((HP - FULL - left, 128), F32)
+    parts = []
+    for j in range(STRIPS):
+        first = STRIPS * FULL + left * j
+        rest = jnp.concatenate([strips[first : first + left], fill], axis=0)
+        parts.append(jnp.concatenate([strips[FULL * j : FULL * (j + 1)], rest], axis=0))
+    return jnp.concatenate(parts, axis=1)
+
+
 def kernel(
     clean_hbm, noise_hbm, bucket, mod_hbm, w1_hbm, w2_hbm, out1, out2,
     clean, noise, mod, w1_in, w2_in, w1_out, w2_out, w1_got, w2_got,
-    st, tg, s_all, t_all, s_tok, base, wa, wb, ga, gb,
+    st, tg, s_all, t_all, s_tok, base, wa, wb, wa_strips, wb_strips, ga, gb,
     ra1, ra2, rx1, rx2, rb1, rb2, ry1, ry2,
     gain, pre, hid, dpre, raw, raw_out, raw_in, norm_row, norm_in,
     dbr, dbn, dot_rows, dh, zs1, zs2, zr1, zr2, load_sems, send_sems, recv_sems,
@@ -235,19 +263,19 @@
 
     def side_a():
         s = Side()
-        s.w, s.g, s.i1, s.i2 = wa, ga, x, y
+        s.w, s.full, s.g, s.i1, s.i2 = wa_strips, wa, ga, x, y
         s.p1 = lambda d: peer(dx=d)
         s.p2 = lambda d: peer(dy=d)
-        s.cut = 32
+        s.cut = (SIZE_W // 2, SIZE_W // 2)
         s.half1, s.half2, s.full1, s.full2 = rx1, ra1, rx2, ra2
         return s
 
     def side_b():
         s = Side()
-        s.w, s.g, s.i1, s.i2 = wb, gb, y, x
+        s.w, s.full, s.g, s.i1, s.i2 = wb_strips, wb, gb, y, x
         s.p1 = lambda d: peer(dy=d)
         s.p2 = lambda d: peer(dx=d)
-        s.cut = 16
+        s.cut = (SIZE_W // 2, SIZE_G // 2)
         s.half1, s.half2, s.full1, s.full2 = ry1, rb1, ry2, rb2
         return s
 
@@ -270,7 +298,9 @@
         parts = []
         for q in range(ROWS):
             parts += [unfold(got[q].astype(F32)), fill]
-        s.w[s.i2, s.i1] = jnp.concatenate(parts, axis=1).astype(BF16)
+        whole = jnp.concatenate(parts, axis=1)
+        s.full[s.i2, s.i1] = whole.astype(BF16)
+        pack(whole, s.w, (s.i2, s.i1))
         block = s.w.at[s.i2, s.i1]
         s.first = {d: send(block, block, s.p1(d)) for d in (1, 3)}
         s.second = {}
@@ -278,10 +308,10 @@
 
     for s in (a, b):
         s.first[1].wait_recv()
-        block = s.w.at[s.i2, at1(s, 3), pl.ds(0, s.cut)]
+        block = s.w.at[s.i2, at1(s, 3), pl.ds(0, s.cut[0])]
         s.far_up = send(block, block, s.p1(1))
         s.first[3].wait_recv()
-        block = s.w.at[s.i2, at1(s, 1), pl.ds(s.cut, HP - s.cut)]
+        block = s.w.at[s.i2, at1(s, 1), pl.ds(s.cut[0], s.cut[0])]
         s.far_down = send(block, block, s.p1(3))
         spread_out(s, 3)
         spread_out(s, 1)
@@ -298,6 +328,11 @@
     for d in (2, 1, 3):
         s_copies[d + 4].wait_recv()
 
+    def spread(s, slab, blocks):
+        for d in blocks:
+            at = (slab, at1(s, d))
+            s.full[at] = unpack(s.w[at].astype(F32)).astype(BF16)
+
     def first_half(slab):
         weights = wa[slab].reshape(4 * HP, CP)
         value = dot(weights, s_all[...].reshape(CP, PIX), NN).reshape(4, HP, PIX)
@@ -310,6 +345,7 @@
             hidden = act * jax.nn.sigmoid(act) * SILU_GAIN * gain[slab * 4 + j]
             hid[j * 4 + slab] = hidden.astype(BF16)
 
+    spread(a, y, (1, 2, 3))
     first_half(y)
     s_tok[...] = s_all[...].reshape(CP, PIX).T
 
@@ -340,9 +376,11 @@
 
     for d in (3, 2):
         a.second[d][1].wait_recv()
+    spread(a, at2(a, 3), range(4))
     first_half(at2(a, 3))
     for d in (0, 1):
         a.second[d][3].wait_recv()
+    spread(a, at2(a, 1), range(4))
     first_half(at2(a, 1))
     t_own.wait_recv()
     for d in (2, 1, 3):
@@ -352,9 +390,13 @@
         b.second[d][1].wait_recv()
     for d in (0, 1):
         b.second[d][3].wait_recv()
+    spread(b, x, (1, 2, 3))
+    spread(b, at2(b, 1), range(4))
+    spread(b, at2(b, 3), range(4))
     squares = squares_of(x) + squares_of(at2(b, 1)) + squares_of(at2(b, 3))
     for d in (0, 3, 1, 2):
         a.far[d].wait_recv()
+    spread(a, at2(a, 2), range(4))
     first_half(at2(a, 2))
     def branch(slab, cols):
         weights = wb[slab, :, :, cols].reshape(4 * HP, cols.stop - cols.start)
@@ -365,6 +407,7 @@
         raw[:, cols] = branch(x, cols) + branch(at2(b, 1), cols) + branch(at2(b, 3), cols)
     for d in (0, 3, 1, 2):
         b.far[d].wait_recv()
+    spread(b, at2(b, 2), range(4))
     raw_copies = []
     for cut in CUTS:
         cols = slice(*cut)
@@ -396,17 +439,14 @@
         dot_rows[:, cols] = jnp.broadcast_to(
             jnp.sum(sums, axis=0, keepdims=True), (8, high - low)
         )
-    dot_high = dot_rows[0:1].astype(BF16).astype(F32)
-    dot_low = dot_rows[0:1] - dot_high
     row = lax.broadcasted_iota(jnp.int32, (HP, 1), 0)
 
     def second_grad(slab):
         value = dot(hid[pl.ds(slab * 4, 4)].reshape(4 * HP, PIX), dbr[...], NN)
         for j in range(4):
             block = value[j * HP : (j + 1) * HP]
-            block = jnp.where(row == HALF, dot_high, block)
-            block = jnp.where(row == HALF + 1, dot_low, block)
-            gb[slab, j] = block.astype(BF16)
+            block = jnp.where(row == HALF, dot_rows[0:1], block)
+            pack(block, gb, (slab, j))
 
     def first_grad(slab):
         for j in range(4):
@@ -416,7 +456,8 @@
             grad = dh[j * 4 + slab]
             dpre[j] = (grad * gain[slab * 4 + j] * slope * SILU_GAIN).astype(BF16)
         value = dot(dpre[...].reshape(4 * HP, PIX), s_tok[...], NN)
-        ga[slab] = value.reshape(4, HP, CP).astype(BF16)
+        for j in range(4):
+            pack(value[j * HP : (j + 1) * HP], ga, (slab, j))
 
     def hidden_grad(i, _):
         dh[pl.ds(i * 4, 4)] = dot(wb[i].reshape(4 * HP, CP), dbn[...], NT).reshape(4, HP, PIX)
@@ -454,18 +495,20 @@
 
     def ring_far(s):
         spot = s.g.at[s.i2, at1(s, 2)]
-        low, high = pl.ds(0, s.cut), pl.ds(s.cut, HP - s.cut)
+        low, high = pl.ds(0, s.cut[1]), pl.ds(s.cut[1], s.cut[1])
         s.far_up = send(spot.at[low], s.half1.at[low], s.p1(1))
         s.far_down = send(spot.at[high], s.half1.at[high], s.p1(3))
 
     def ring_near(s, d):
-        low, high = pl.ds(0, s.cut), pl.ds(s.cut, HP - s.cut)
+        low, high = pl.ds(0, s.cut[1]), pl.ds(s.cut[1], s.cut[1])
         part, way = (high, 0) if d == 1 else (low, 1)
         s.near.append(send(s.g.at[s.i2, at1(s, d), part], s.full1.at[way, part], s.p1(d)))
 
     def ring_relay(s, d):
         part, way, copy = (
-            (slice(0, s.cut), 0, s.far_up) if d == 1 else (slice(s.cut, HP), 1, s.far_down)
+            (slice(0, s.cut[1]), 0, s.far_up)
+            if d == 1
+            else (slice(s.cut[1], 2 * s.cut[1]), 1, s.far_down)
         )
         copy.wait_recv()
         at = at1(s, d)
@@ -503,14 +546,14 @@
         ]
 
     def finish_second():
-        grad2 = ring_sum(b)
+        grad2 = unpack(ring_sum(b))
         w2 = wb[x, y].astype(F32)
         inv2 = norm_row[1][0:1]
-        dot2 = grad2[HALF : HALF + 1] + grad2[HALF + 1 : HALF + 2]
+        dot2 = grad2[HALF : HALF + 1]
         return hand_out(grad2 * inv2 - w2 * (dot2 * inv2 * inv2 * inv2), zs2, zr2)
 
     def finish_first():
-        grad1 = ring_sum(a)
+        grad1 = unpack(ring_sum(a))
         w1 = wa[y, x].astype(F32)
         inv1 = lax.rsqrt(jnp.sum(w1 * w1, axis=1, keepdims=True) + 1.0)
         dot1 = jnp.sum(w1 * grad1, axis=1, keepdims=True)
@@ -577,16 +620,18 @@
             pltpu.VMEM((PIX, CP), F32),
             pltpu.VMEM((4, 4, *block), BF16),
             pltpu.VMEM((4, 4, *block), BF16),
-            pltpu.VMEM((4, 4, *block), BF16),
-            pltpu.VMEM((4, 4, *block), BF16),
-            pltpu.VMEM((4, *block), BF16),
-            pltpu.VMEM((2, 4, *block), BF16),
-            pltpu.VMEM(block, BF16),
-            pltpu.VMEM((2, *block), BF16),
-            pltpu.VMEM((4, *block), BF16),
-            pltpu.VMEM((2, 4, *block), BF16),
-            pltpu.VMEM(block, BF16),
-            pltpu.VMEM((2, *block), BF16),
+            pltpu.VMEM((4, 4, SIZE_W, 128), BF16),
+            pltpu.VMEM((4, 4, SIZE_W, 128), BF16),
+            pltpu.VMEM((4, 4, SIZE_W, 128), BF16),
+            pltpu.VMEM((4, 4, SIZE_G, 128), BF16),
+            pltpu.VMEM((4, SIZE_W, 128), BF16),
+            pltpu.VMEM((2, 4, SIZE_W, 128), BF16),
+            pltpu.VMEM((SIZE_W, 128), BF16),
+            pltpu.VMEM((2, SIZE_W, 128), BF16),
+            pltpu.VMEM((4, SIZE_G, 128), BF16),
+            pltpu.VMEM((2, 4, SIZE_G, 128), BF16),
+            pltpu.VMEM((SIZE_G, 128), BF16),
+            pltpu.VMEM((2, SIZE_G, 128), BF16),
             pltpu.VMEM((16, HP, PIX), F32),
             pltpu.VMEM((16, HP, PIX), F32),
             pltpu.VMEM((16, HP, PIX), BF16),

time: 80 us -> 75.3 us (0.941)
  Pallas kernels: 76.9 us -> 72.2 us
    pallas_call x1, Pallas kernels: 76.9 us -> 72.2 us  [local(): pl.pallas_call(kernel, out_shape=(jax.ShapeDtypeStruct((1, CHAN, BLOCK),...]
where the time goes in v5:
time: 75.3 us; the launch traced here: 75.2 us
  Pallas kernels  72.2 us (96%)
  other arithmetic  2.27 us (3%)
    pallas_call x1, Pallas kernels, local(): pl.pallas_call(kernel, out_shape=(jax.ShapeDtypeStruct((1, CHAN, BLOCK),...  72.2 us
    div x1, other arithmetic, local(): return (first / SAMPLES, jnp.transpose(second / SAMPLES, (1, 0, 2)))  1.56 us

profile of v5, /device:TPU:1, one launch (start us, length us, event | category | flops | bytes accessed | tf_op | source)
XLA Modules:
  0.0 75.2 jit_solution(17574262139598561668)
XLA Ops:
  0.6 72.2 %shard_map.77 = (f32[1,168,84]{2,1,0:T(8,128)}, f32[84,1,168]{2,1,0:T(1,128)}) custom-call(f32[168,1024]{1,0:T(8,128)} %clean_hbm.1, f32[168,1024]{1,0:T(8,128)} %noise_hbm.1, s32[64]{0:T(128)} %bucket.1, f32[1,32,1344]{2,1,0:T(8,128)} %mod_hbm.1, f32[1,168,84]{2,1,0:T(8,128)} %w1_hbm.1, f32[84,1,168]{2,1,0:T(1,128)} %bitcast.3), custom_call_target="tpu_custom_call" | custom-call | tf_op jit(solution)/shard_map/pallas_call | solution.py:597
  72.9 0.0 copy-start
  72.9 1.6 %broadcast_multiply_fusion = f32[1,168,84]{2,1,0:T(8,128)} fusion(f32[1,168,84]{2,1,0:T(8,128)} %get-tuple-element.4), kind=kLoop, calls=%fused_computation.1 | loop fusion | flops 14112 | bytes 112896 | tf_op jit(solution)/shard_map/div | solution.py:660
  74.5 0.0 copy-done
  74.5 0.7 multiply_bitcast_fusion
Async XLA Ops:
  72.9 1.6 %copy-start = (f32[84,1,168]{2,1,0:T(1,128)S(1)}, f32[84,1,168]{2,1,0:T(1,128)}, u32[]{:S(2)}) copy-start(f32[84,1,168]{2,1,0:T(1,128)} %get-tuple-element.5) | copy-start | bytes 169348
